TPU v7x, 32 devices: a whole 2x2x4 slice. The times are simulated.
32 devices in a mesh: ba: 4 (over x, core), ma: 4 (over z), row: 2 (over y).
Axes of the slice: x: 2, y: 2, z: 4, core: 2. Of those that a mesh axis runs over, the one named last changes fastest.
Arguments:
- tokens: bfloat16 [8, 256, 4096], P(('ba', 'row'), None, 'ma'), may hold values from -6 to 6
- attn_gain: bfloat16 [4096], P('ma'), may hold values from 0.25 to 1.75
- query_weight: bfloat16 [4096, 4096], P('row', 'ma'), may hold values from -0.046875 to 0.046875
- key_weight: bfloat16 [4096, 4096], P('row', 'ma'), may hold values from -0.046875 to 0.046875
- value_projection_matrix: bfloat16 [4096, 4096], P('row', 'ma'), may hold values from -0.09375 to 0.09375
- attention_output_matrix: bfloat16 [4096, 4096], P('ma', 'row'), may hold values from -0.125 to 0.125
- bucket_bias_matrix: float32 [32, 64], P(None, 'ma'), may hold values from -6 to 215, as said below
- ffn_gain: bfloat16 [4096], P('ma'), may hold values from 0.25 to 1.75
- gate_weight: bfloat16 [4096, 8192], P(None, ('ma', 'row')), may hold values from -0.09375 to 0.09375
- up_weight: bfloat16 [4096, 8192], P(None, ('ma', 'row')), may hold values from -0.09375 to 0.09375
- down_projection_weight: bfloat16 [8192, 4096], P(('ma', 'row')), may hold values from -0.09375 to 0.09375
Outputs:
- encoded: bfloat16 [8, 256, 4096], P(('ba', 'row'), None, 'ma')
Inputs may be any that keep to these rules, and one draw needn't show every extreme that they name: `bucket_bias_matrix`: entries of the relative position table.
All inputs are finite; a program needn't handle non-finite values.
Results may differ from a plain program's by a relative error of at most 0.017.
Values may be sent and summed in bfloat16 or wider, within the bound.
A program may use at most 128 MiB of HBM per device.

v0:
```python
import jax
import jax.numpy as jnp
from jax import lax
from jax.sharding import PartitionSpec as P

bucket_thresholds = (1, 2, 3, 4, 5, 6, 7, 8, 11, 16, 23, 32, 45, 64, 91, 128)
epsilon = 1e-06


def buckets(length):
    places = jnp.arange(length, dtype=jnp.int32)
    offset = places[None, :] - places[:, None]
    distance = jnp.abs(offset)
    backward = jnp.zeros_like(distance)
    for threshold in bucket_thresholds[:15]:
        backward = backward + (distance >= threshold).astype(jnp.int32)
    forward = jnp.full_like(distance, 15)
    for threshold in bucket_thresholds:
        forward = forward + (distance >= threshold).astype(jnp.int32)
    return jnp.where(offset > 0, forward, backward)


def rms_scale(values, gain):
    mean_square = jnp.mean(values * values, axis=-1, keepdims=True)
    return (values * lax.rsqrt(mean_square + epsilon) * gain.astype(jnp.float32)).astype(
        jnp.bfloat16
    )


def regroup(values, norm_gain_vector):
    widened = (
        lax.all_gather(values, "ma", axis=1, tiled=True),
        lax.all_gather(norm_gain_vector, "ma", axis=1, tiled=True),
    )
    stacked = lax.all_gather(widened[0], "row", axis=0, tiled=True)
    return (stacked, widened[1])


def on_device(
    tokens,
    attn_gain,
    query_weight,
    key_weight,
    value_projection_matrix,
    attention_output_matrix,
    bucket_bias_matrix,
    ffn_gain,
    gate_weight,
    up_weight,
    down_projection_weight,
):
    sequences, length, part_width = tokens.shape
    ma_count = lax.axis_size("ma")
    local_heads = bucket_bias_matrix.shape[1]
    inner_width = query_weight.shape[1]
    head_size = inner_width // local_heads
    slab_rows = sequences * length
    token_rows = tokens.reshape(slab_rows, part_width)
    token_float = token_rows.astype(jnp.float32)
    full_weights = (
        lax.all_gather(query_weight, "row", axis=0, tiled=True),
        lax.all_gather(key_weight, "row", axis=0, tiled=True),
        lax.all_gather(value_projection_matrix, "row", axis=0, tiled=True),
    )
    whole_rows, whole_gain = (
        lax.all_gather(token_rows, "ma", axis=1, tiled=True),
        lax.all_gather(attn_gain.reshape(1, part_width), "ma", axis=1, tiled=True),
    )
    normed = rms_scale(whole_rows.astype(jnp.float32), whole_gain[0])
    projected = tuple(
        (jnp.dot(normed, matrix, preferred_element_type=jnp.float32) for matrix in full_weights)
    )
    query_heads, key_heads, value_heads = [
        member.astype(jnp.bfloat16).reshape(sequences, length, local_heads, head_size)
        for member in projected
    ]
    bucket_grid = buckets(length)
    table_rows = jnp.arange(bucket_bias_matrix.shape[0], dtype=jnp.int32)
    bucket_indicator = (table_rows[:, None, None] == bucket_grid[None, :, :]).astype(jnp.float32)
    relative_position_scores = jnp.einsum(
        "dmy,du->umy", bucket_indicator, bucket_bias_matrix, precision=lax.Precision.HIGHEST
    )
    scores = (
        jnp.einsum("sqhd,skhd->shqk", query_heads, key_heads, preferred_element_type=jnp.float32)
        + relative_position_scores[None]
    )
    row_max = jnp.max(scores, axis=-1, keepdims=True)
    exponent = jnp.exp(scores - row_max)
    weights = (exponent / jnp.sum(exponent, axis=-1, keepdims=True)).astype(jnp.bfloat16)
    attended = jnp.einsum(
        "shqk,skhd->sqhd", weights, value_heads, preferred_element_type=jnp.float32
    )
    attended = attended.astype(jnp.bfloat16).reshape(slab_rows, inner_width)
    partial_out = jnp.dot(
        attended,
        lax.all_gather(attention_output_matrix, "row", axis=1, tiled=True),
        preferred_element_type=jnp.float32,
    )
    attn_out = lax.psum_scatter(
        partial_out.astype(jnp.bfloat16), "ma", scatter_dimension=1, tiled=True
    ).astype(jnp.float32)
    residual_stream = (token_float + attn_out).astype(jnp.bfloat16)
    residual_f = residual_stream.astype(jnp.float32)
    norm_gain_vector = ffn_gain.reshape(1, part_width)
    gate_full, up_full, down_full = (gate_weight, up_weight, down_projection_weight)
    group_rows, group_gain = regroup(residual_stream, norm_gain_vector)
    ffn_in = rms_scale(group_rows.astype(jnp.float32), group_gain[0])
    gate_act = jnp.dot(ffn_in, gate_full, preferred_element_type=jnp.float32)
    up_act = jnp.dot(ffn_in, up_full, preferred_element_type=jnp.float32)
    hidden = (jax.nn.gelu(gate_act, approximate=True) * up_act).astype(jnp.bfloat16)
    down_blocks = down_full.reshape(down_full.shape[0], ma_count, part_width)
    down_terms = jnp.einsum("tf,fmd->mtd", hidden, down_blocks, preferred_element_type=jnp.float32)
    down_terms = down_terms.reshape(ma_count * ffn_in.shape[0], part_width)
    ffn_out = lax.psum_scatter(
        down_terms.astype(jnp.bfloat16), ("ma", "row"), scatter_dimension=0, tiled=True
    ).astype(jnp.float32)
    encoded = (residual_f + ffn_out).astype(jnp.bfloat16)
    return encoded.reshape(sequences, length, part_width)


def solution(mesh):
    in_specs = (
        P(("ba", "row"), None, "ma"),
        P("ma"),
        P("row", "ma"),
        P("row", "ma"),
        P("row", "ma"),
        P("ma", "row"),
        P(None, "ma"),
        P("ma"),
        P(None, ("ma", "row")),
        P(None, ("ma", "row")),
        P(("ma", "row"), None),
    )
    out_specs = P(("ba", "row"), None, "ma")
    return jax.shard_map(
        on_device, mesh=mesh, in_specs=in_specs, out_specs=out_specs, check_vma=False
    )
```

profile of v0, /device:TPU:0, one launch (start us, length us, event | category | flops | bytes accessed | tf_op | source)
XLA Modules:
  0.0 752.7 jit_solution(16300057747724244085)
XLA Ops:
  6.5 0.7 all-gather.23.cloned.1.call-update
  7.3 0.7 all-gather.13.cloned.1.call-update
  10.0 13.7 %all-gather.1 = bf16[4096]{0:T(1024)(128)(2,1)S(1)} all-gather(bf16[1024]{0:T(1024)(128)(2,1)S(1)} %copy-done.7), channel_id=3, replica_groups=mesh['ba'=4,'ma'=4,'row'=2] {'ma'}, dimensions={0}, use_global_device_ids=true | all-gather | bytes 10240 | tf_op jit(solution)/shard_map/all_gather | solution.py:67
  24.1 4.2 fusion.7
  28.3 5.3 copy.27
  33.6 23.8 %all-gather.23.cloned.1.call-done = bf16[1,256,4096]{2,1,0:T(8,128)(2,1)} async-done(((bf16[1,256,1024]{2,1,0:T(8,128)(2,1)}), bf16[1,256,4096]{2,1,0:T(8,128)(2,1)}) %all-gather.23.cloned.1.call-update) | async-done | bytes 2097168 | tf_op jit(solution)/shard_map/all_gather | solution.py:66
  57.3 2.1 fusion.8
  59.4 102.2 %all-gather.13.cloned.1.call-done = bf16[4096,1024]{1,0:T(8,128)(2,1)} async-done(((bf16[2048,1024]{1,0:T(8,128)(2,1)}), bf16[4096,1024]{1,0:T(8,128)(2,1)}) %all-gather.13.cloned.1.call-update) | async-done | bytes 8388624 | tf_op jit(solution)/shard_map/all_gather | solution.py:61
  161.7 6.4 convolution_convert_fusion.2
  168.3 99.0 %all-gather.15.cloned.1.call-done = bf16[4096,1024]{1,0:T(8,128)(2,1)} async-done(((bf16[2048,1024]{1,0:T(8,128)(2,1)}), bf16[4096,1024]{1,0:T(8,128)(2,1)}) %all-gather.15.cloned.1.call-update) | async-done | bytes 8388624 | tf_op jit(solution)/shard_map/all_gather | solution.py:62
  267.3 6.6 convolution_convert_fusion.1
  273.9 1.3 copy.26
  275.2 97.5 %all-gather.11.cloned.1.call-done = bf16[4096,1024]{1,0:T(8,128)(2,1)} async-done(((bf16[2048,1024]{1,0:T(8,128)(2,1)}), bf16[4096,1024]{1,0:T(8,128)(2,1)}) %all-gather.11.cloned.1.call-update) | async-done | bytes 8388624 | tf_op jit(solution)/shard_map/all_gather | solution.py:63
  372.7 6.6 convolution_convert_fusion.3
  379.3 1.3 copy.24
  380.6 3.6 bitcast_add_fusion
  384.3 2.0 copy-done.2
  386.3 0.8 fusion.57
  387.1 5.3 fusion.26
  392.3 85.8 %all-gather.17.cloned.1.call-done = bf16[1024,4096]{1,0:T(8,128)(2,1)} async-done(((bf16[1024,2048]{1,0:T(8,128)(2,1)}), bf16[1024,4096]{1,0:T(8,128)(2,1)}) %all-gather.17.cloned.1.call-update) | async-done | bytes 8388624 | tf_op jit(solution)/shard_map/all_gather | solution.py:96
  478.1 7.2 convolution_convert_fusion
  485.4 43.7 %reduce-scatter.3.cloned.1.call-done = bf16[256,1024]{1,0:T(8,128)(2,1)} async-done(((bf16[256,4096]{1,0:T(8,128)(2,1)}), bf16[256,1024]{1,0:T(8,128)(2,1)}) %reduce-scatter.3.cloned.1.call-update) | async-done | bytes 524304 | tf_op jit(solution)/shard_map/reduce_scatter | solution.py:99
  529.1 2.0 fusion.30
  531.2 45.0 %all-gather.19.cloned.1.call-done = bf16[256,4096]{1,0:T(8,128)(2,1)} async-done(((bf16[256,1024]{1,0:T(8,128)(2,1)}), bf16[256,4096]{1,0:T(8,128)(2,1)}) %all-gather.19.cloned.1.call-update) | async-done | bytes 2097168 | tf_op jit(solution)/shard_map/all_gather | solution.py:32
  576.3 12.2 %all-gather.2 = bf16[4096]{0:T(1024)(128)(2,1)S(1)} all-gather(bf16[1024]{0:T(1024)(128)(2,1)S(1)} %copy-done.8), channel_id=4, replica_groups=mesh['ba'=4,'ma'=4,'row'=2] {'ma'}, dimensions={0}, use_global_device_ids=true | all-gather | bytes 10240 | tf_op jit(solution)/shard_map/all_gather | solution.py:33
  588.5 44.9 %all-gather.21.cloned.1.call-done = bf16[512,4096]{1,0:T(8,128)(2,1)} async-done(((bf16[256,4096]{1,0:T(8,128)(2,1)}), bf16[512,4096]{1,0:T(8,128)(2,1)}) %all-gather.21.cloned.1.call-update) | async-done | bytes 4194320 | tf_op jit(solution)/shard_map/all_gather | solution.py:35
  633.3 3.2 fusion.1
  636.8 7.7 %fusion.28 = f32[512,1024]{1,0:T(8,128)S(1)} fusion(bf16[4096,1024]{1,0:T(8,128)(2,1)} %param.19, bf16[512,4096]{1,0:T(8,128)(2,1)S(1)} %copy-done.4, f32[4096]{0:T(1024)S(1)} %mul.97, f32[512]{0:T(512)S(1)} %add_rsqrt_fusion), kind=kOutput, calls=%fused_computation.38 | convolution fusion | flops 4303355904 | bytes 14698496 | tf_op jit(solution)/shard_map/dot_general | solution.py:108
  644.6 4.9 fusion.25
  649.5 6.2 fusion.12
  655.6 88.5 %reduce-scatter.5.cloned.1.call-done = bf16[256,1024]{1,0:T(8,128)(2,1)} async-done(((bf16[2048,1024]{1,0:T(8,128)(2,1)}), bf16[256,1024]{1,0:T(8,128)(2,1)}) %reduce-scatter.5.cloned.1.call-update) | async-done | bytes 524304 | tf_op jit(solution)/shard_map/reduce_scatter | solution.py:114
  744.1 2.0 fusion.31
  (49 shorter events, 2.9 us)
Async XLA Ops:
  6.5 17.5 %copy-start = (f32[32,16]{0,1:T(8,128)S(1)}, f32[32,16]{0,1:T(8,128)}, u32[]{:S(2)}) copy-start(f32[32,16]{0,1:T(8,128)} %param.17) | copy-start | bytes 6148
  6.5 50.8 %all-gather.23.cloned.1.call-start = ((), (), s32[]{:S(2)}) async-start(), calls=%async_computation.10 | async-start | bytes 2621440 | tf_op jit(solution)/shard_map/all_gather | solution.py:66
  7.3 154.4 %all-gather.13.cloned.1.call-start = ((), (), s32[]{:S(2)}) async-start(), calls=%async_computation.3 | async-start | bytes 12582912 | tf_op jit(solution)/shard_map/all_gather | solution.py:61
  8.0 259.3 %all-gather.15.cloned.1.call-start = ((), (), s32[]{:S(2)}) async-start(), calls=%async_computation.4 | async-start | bytes 12582912 | tf_op jit(solution)/shard_map/all_gather | solution.py:62
  8.7 1.2 copy-start.7
  8.8 363.9 %all-gather.11.cloned.1.call-start = ((), (), s32[]{:S(2)}) async-start(), calls=%async_computation.2 | async-start | bytes 12582912 | tf_op jit(solution)/shard_map/all_gather | solution.py:63
  9.3 468.8 %all-gather.17.cloned.1.call-start = ((), (), s32[]{:S(2)}) async-start(), calls=%async_computation.5 | async-start | bytes 12582912 | tf_op jit(solution)/shard_map/all_gather | solution.py:96
  9.9 519.2 %reduce-scatter.3.cloned.1.call-start = ((), (), s32[]{:S(2)}) async-start(), calls=%async_computation.6 | async-start | bytes 2621440 | tf_op jit(solution)/shard_map/reduce_scatter | solution.py:99
  59.4 207.9 %copy-start.6 = (bf16[1,256,4096]{2,1,0:T(8,128)(2,1)S(1)}, bf16[1,256,4096]{2,1,0:T(8,128)(2,1)}, u32[]{:S(2)}) copy-start(bf16[1,256,4096]{2,1,0:T(8,128)(2,1)} %all-gather.23.cloned.1.call-done) | copy-start | bytes 6291460
  384.3 2.1 copy-start.2
  478.1 51.0 %copy-start.5 = (bf16[1,256,1024]{2,1,0:T(8,128)(2,1)S(1)}, bf16[1,256,1024]{2,1,0:T(8,128)(2,1)}, u32[]{:S(2)}) copy-start(bf16[1,256,1024]{2,1,0:T(8,128)(2,1)} %param.11) | copy-start | bytes 1572868
  485.3 91.0 %copy-start.8 = (bf16[1024]{0:T(1024)(128)(2,1)S(1)}, bf16[1024]{0:T(1024)(128)(2,1)}, u32[]{:S(2)}) copy-start(bf16[1024]{0:T(1024)(128)(2,1)} %param.18) | copy-start | bytes 6148
  485.4 90.9 %all-gather.19.cloned.1.call-start = ((), (), s32[]{:S(2)}) async-start(), calls=%async_computation.7 | async-start | bytes 2621440 | tf_op jit(solution)/shard_map/all_gather | solution.py:32
  531.2 102.1 %all-gather.21.cloned.1.call-start = ((), (), s32[]{:S(2)}) async-start(), calls=%async_computation.8 | async-start | bytes 6291456 | tf_op jit(solution)/shard_map/all_gather | solution.py:35
  576.2 167.9 %reduce-scatter.5.cloned.1.call-start = ((), (), s32[]{:S(2)}) async-start(), calls=%async_computation.9 | async-start | bytes 4718592 | tf_op jit(solution)/shard_map/reduce_scatter | solution.py:114
  633.3 3.4 copy-start.4
  633.3 11.2 %slice-start = ((s8[8388608]{0:T(1024)(128)(4,1)}), s8[4194304]{0:T(1024)(128)(4,1)S(1)}, s32[]{:S(2)}) async-start(s8[8388608]{0:T(1024)(128)(4,1)} %bitcast.54), calls=%async_computation.11 | async-start | bytes 8388608
  633.3 16.1 %slice-start.2 = ((s8[8388608]{0:T(1024)(128)(4,1)}), s8[4194304]{0:T(1024)(128)(4,1)S(1)}, s32[]{:S(2)}) async-start(s8[8388608]{0:T(1024)(128)(4,1)} %bitcast.56), calls=%async_computation.13 | async-start | bytes 8388608
  636.8 7.8 %slice-start.1 = ((s8[8388608]{0:T(1024)(128)(4,1)}), s8[4194304]{0:T(1024)(128)(4,1)S(1)}, s32[]{:S(2)}) async-start(s8[8388608]{0:T(1024)(128)(4,1)} %bitcast.54), calls=%async_computation.12 | async-start | bytes 8388608
  636.8 12.7 %slice-start.3 = ((s8[8388608]{0:T(1024)(128)(4,1)}), s8[4194304]{0:T(1024)(128)(4,1)S(1)}, s32[]{:S(2)}) async-start(s8[8388608]{0:T(1024)(128)(4,1)} %bitcast.56), calls=%async_computation.14 | async-start | bytes 8388608
  649.5 96.7 %copy-start.1 = (f32[32,16]{0,1:T(8,128)S(1)}, f32[32,16]{0,1:T(8,128)}, u32[]{:S(2)}) copy-start(f32[32,16]{0,1:T(8,128)} %param.17) | copy-start | bytes 6148
  655.6 88.5 %copy-start.3 = (bf16[256,1024]{1,0:T(8,128)(2,1)S(1)}, bf16[256,1024]{1,0:T(8,128)(2,1)}, u32[]{:S(2)}) copy-start(bf16[256,1024]{1,0:T(8,128)(2,1)} %fusion.30) | copy-start | bytes 1572868
Sparse Core Ops, SparseCore 0:
  8.9 48.3 all-gather.22
  58.9 102.7 all-gather.12
  163.2 104.0 all-gather.14
  268.7 103.9 all-gather.10
  374.1 103.9 all-gather.16
  485.5 43.6 reduce-scatter.2
  531.3 44.8 all-gather.18
  577.8 55.5 all-gather.20
  655.8 88.3 reduce-scatter.4
where the time goes:
time: 753 us
  waiting for transfers between devices  634 us (84%)
  matrix products  58.6 us (8%)
  blocking collectives  25.9 us (3%)
  between operations  13.4 us (2%)
  other arithmetic  10.5 us (1%)
  local copies, waits for them, and re-layouts  10.4 us (1%)
    all_gather x1, waiting for transfers between devices, on_device(): lax.all_gather(query_weight, 'row', axis=0, tiled=True)  102 us
    all_gather x1, waiting for transfers between devices, on_device(): lax.all_gather(key_weight, 'row', axis=0, tiled=True)  99 us
    all_gather x1, waiting for transfers between devices, on_device(): lax.all_gather(value_projection_matrix, 'row', axis=0, tiled=True)  97.5 us
    reduce_scatter x1, waiting for transfers between devices, on_device(): lax.psum_scatter(down_terms.astype(jnp.bfloat16), ('ma', 'row'), scatter_...  88.5 us
    all_gather x1, waiting for transfers between devices, on_device(): lax.all_gather(attention_output_matrix, 'row', axis=1, tiled=True)  85.8 us
    all_gather x1, waiting for transfers between devices, regroup(): lax.all_gather(values, 'ma', axis=1, tiled=True)  45 us
    all_gather x1, waiting for transfers between devices, regroup(): stacked = lax.all_gather(widened[0], 'row', axis=0, tiled=True)  44.9 us
    reduce_scatter x1, waiting for transfers between devices, on_device(): lax.psum_scatter(partial_out.astype(jnp.bfloat16), 'ma', scatter_dimensio...  43.7 us
  transfers between devices with their start and end apart: 9, of which 9 were waited for; matrix products, arithmetic and copies ran while one was open for 6% of the time, Pallas kernels for 0%

commit v1 on v0

--- a/solution.py
+++ b/solution.py
@@ -27,15 +27,6 @@
     )
 
 
-def regroup(values, norm_gain_vector):
-    widened = (
-        lax.all_gather(values, "ma", axis=1, tiled=True),
-        lax.all_gather(norm_gain_vector, "ma", axis=1, tiled=True),
-    )
-    stacked = lax.all_gather(widened[0], "row", axis=0, tiled=True)
-    return (stacked, widened[1])
-
-
 def on_device(
     tokens,
     attn_gain,
@@ -57,19 +48,31 @@
     slab_rows = sequences * length
     token_rows = tokens.reshape(slab_rows, part_width)
     token_float = token_rows.astype(jnp.float32)
-    full_weights = (
-        lax.all_gather(query_weight, "row", axis=0, tiled=True),
-        lax.all_gather(key_weight, "row", axis=0, tiled=True),
-        lax.all_gather(value_projection_matrix, "row", axis=0, tiled=True),
+    row_count = lax.axis_size("row")
+    half = query_weight.shape[0]
+    swap = [(i, i ^ 1) for i in range(row_count)]
+    my_row = lax.axis_index("row")
+    gains = jnp.concatenate(
+        [attn_gain.reshape(1, part_width), ffn_gain.reshape(1, part_width)]
+        + [jnp.zeros((14, part_width), jnp.bfloat16)]
     )
-    whole_rows, whole_gain = (
-        lax.all_gather(token_rows, "ma", axis=1, tiled=True),
-        lax.all_gather(attn_gain.reshape(1, part_width), "ma", axis=1, tiled=True),
-    )
-    normed = rms_scale(whole_rows.astype(jnp.float32), whole_gain[0])
-    projected = tuple(
-        (jnp.dot(normed, matrix, preferred_element_type=jnp.float32) for matrix in full_weights)
-    )
+    whole = lax.all_gather(jnp.concatenate([token_rows, gains]), "ma", axis=1, tiled=True)
+    whole_rows = whole[:slab_rows]
+    ffn_gain_full = whole[slab_rows + 1]
+    normed = rms_scale(whole_rows.astype(jnp.float32), whole[slab_rows])
+    mine = lax.dynamic_slice_in_dim(normed, my_row * half, half, 1)
+    theirs = lax.dynamic_slice_in_dim(normed, (1 - my_row) * half, half, 1)
+    arrived = lax.ppermute(theirs, "row", swap)
+    weights_qkv = (query_weight, key_weight, value_projection_matrix)
+    outgoing = [
+        jnp.dot(arrived, matrix, preferred_element_type=jnp.float32).astype(jnp.bfloat16)
+        for matrix in weights_qkv
+    ]
+    incoming = [lax.ppermute(part, "row", swap) for part in outgoing]
+    projected = [
+        jnp.dot(mine, matrix, preferred_element_type=jnp.float32) + part.astype(jnp.float32)
+        for matrix, part in zip(weights_qkv, incoming)
+    ]
     query_heads, key_heads, value_heads = [
         member.astype(jnp.bfloat16).reshape(sequences, length, local_heads, head_size)
         for member in projected
@@ -91,20 +94,29 @@
         "shqk,skhd->sqhd", weights, value_heads, preferred_element_type=jnp.float32
     )
     attended = attended.astype(jnp.bfloat16).reshape(slab_rows, inner_width)
-    partial_out = jnp.dot(
-        attended,
-        lax.all_gather(attention_output_matrix, "row", axis=1, tiled=True),
-        preferred_element_type=jnp.float32,
+    attended_peer = lax.ppermute(attended, "row", swap)
+    sent_out = jnp.dot(
+        attended_peer, attention_output_matrix, preferred_element_type=jnp.float32
+    ).astype(jnp.bfloat16)
+    other_half = lax.ppermute(sent_out, "row", swap)
+    own_half = jnp.dot(
+        attended, attention_output_matrix, preferred_element_type=jnp.float32
+    ).astype(jnp.bfloat16)
+    partial_out = jnp.where(
+        my_row == 0,
+        jnp.concatenate([own_half, other_half], axis=1),
+        jnp.concatenate([other_half, own_half], axis=1),
     )
     attn_out = lax.psum_scatter(
         partial_out.astype(jnp.bfloat16), "ma", scatter_dimension=1, tiled=True
     ).astype(jnp.float32)
     residual_stream = (token_float + attn_out).astype(jnp.bfloat16)
     residual_f = residual_stream.astype(jnp.float32)
-    norm_gain_vector = ffn_gain.reshape(1, part_width)
     gate_full, up_full, down_full = (gate_weight, up_weight, down_projection_weight)
-    group_rows, group_gain = regroup(residual_stream, norm_gain_vector)
-    ffn_in = rms_scale(group_rows.astype(jnp.float32), group_gain[0])
+    group_rows = lax.all_gather(
+        lax.all_gather(residual_stream, "ma", axis=1, tiled=True), "row", axis=0, tiled=True
+    )
+    ffn_in = rms_scale(group_rows.astype(jnp.float32), ffn_gain_full)
     gate_act = jnp.dot(ffn_in, gate_full, preferred_element_type=jnp.float32)
     up_act = jnp.dot(ffn_in, up_full, preferred_element_type=jnp.float32)
     hidden = (jax.nn.gelu(gate_act, approximate=True) * up_act).astype(jnp.bfloat16)

time: 753 us -> 447 us (0.59)
  waiting for transfers between devices: 634 us -> 345 us
  blocking collectives: 25.9 us -> 0 us
  matrix products: 58.6 us -> 47.9 us
  other arithmetic: 10.5 us -> 20.9 us
  starting transfers between devices: 0.31 us -> 8.36 us
    all_gather x7 -> x3, waiting for transfers between devices: 498 us -> 143 us  [the longest x1 56.9 us: on_device(): lax.all_gather(lax.all_gather(residual_stream, 'ma', axis=1, tiled=True),...]
    ppermute x0 -> x6, waiting for transfers between devices: none -> 70.2 us  [the longest x3 25.5 us: on_device(): incoming = [lax.ppermute(part, 'row', swap) for part in outgoing]]
    all_gather x2 -> x0, blocking collectives: 25.9 us -> none  [the longest x1 13.7 us: on_device(): lax.all_gather(attn_gain.reshape(1, part_width), 'ma', axis=1, tiled=True)]
    dot_general x4 -> x8, matrix products: 26.8 us -> 17.5 us  [the longest x3 5.43 us: on_device(): jnp.dot(arrived, matrix, preferred_element_type=jnp.float32)]
    ppermute x0 -> x6, starting transfers between devices: none -> 8.19 us  [the longest x3 3.57 us: on_device(): incoming = [lax.ppermute(part, 'row', swap) for part in outgoing]]
  transfers between devices with their start and end apart: 9 -> 11, of which waited for: 9 -> 11; matrix products, arithmetic and copies ran while one was open for 6% -> 6% of each run, Pallas kernels for 0% -> 0%
where the time goes in v1:
time: 447 us; the launch traced here: 446 us
  waiting for transfers between devices  345 us (77%)
  matrix products  47.9 us (11%)
  other arithmetic  20.9 us (5%)
  between operations  13.4 us (3%)
  local copies, waits for them, and re-layouts  10.5 us (2%)
  starting transfers between devices  8.36 us (2%)
    reduce_scatter x1, waiting for transfers between devices, on_device(): lax.psum_scatter(down_terms.astype(jnp.bfloat16), ('ma', 'row'), scatter_...  88.5 us
    all_gather x1, waiting for transfers between devices, on_device(): lax.all_gather(lax.all_gather(residual_stream, 'ma', axis=1, tiled=True),...  56.9 us
    all_gather x1, waiting for transfers between devices, on_device(): lax.all_gather(residual_stream, 'ma', axis=1, tiled=True)  45 us
    reduce_scatter x1, waiting for transfers between devices, on_device(): lax.psum_scatter(partial_out.astype(jnp.bfloat16), 'ma', scatter_dimensio...  43.6 us
    all_gather x1, waiting for transfers between devices, on_device(): lax.all_gather(jnp.concatenate([token_rows, gains]), 'ma', axis=1, tiled=...  40.9 us
    ppermute x3, waiting for transfers between devices, on_device(): incoming = [lax.ppermute(part, 'row', swap) for part in outgoing]  25.5 us
    ppermute x1, waiting for transfers between devices, on_device(): arrived = lax.ppermute(theirs, 'row', swap)  17.6 us
    ppermute x1, waiting for transfers between devices, on_device(): other_half = lax.ppermute(sent_out, 'row', swap)  16.8 us
  transfers between devices with their start and end apart: 11, of which 11 were waited for; matrix products, arithmetic and copies ran while one was open for 6% of the time, Pallas kernels for 0%

profile of v1, /device:TPU:0, one launch (start us, length us, event | category | flops | bytes accessed | tf_op | source)
XLA Modules:
  0.0 446.0 jit_solution(12807414169357274432)
XLA Ops:
  8.0 2.0 maximum_maximum_fusion
  10.5 4.2 fusion.7
  14.7 5.2 %copy.21 = f32[256,256,16]{0,1,2:T(8,128)} copy(f32[256,256,16]{1,2,0:T(8,128)} %fusion.7) | data formatting | bytes 8388608 | tf_op jit(solution)/shard_map/dmy,du->umy/dot_general | solution.py:83
  19.9 40.9 %all-gather.4.cloned.1.call-done = bf16[272,4096]{1,0:T(8,128)(2,1)} async-done(((bf16[272,1024]{1,0:T(8,128)(2,1)}), bf16[272,4096]{1,0:T(8,128)(2,1)}) %all-gather.4.cloned.1.call-update) | async-done | bytes 2228240 | tf_op jit(solution)/shard_map/all_gather | solution.py:59
  60.8 2.2 fusion.8
  63.9 2.2 fusion.10
  67.8 2.2 fusion.32
  73.5 17.6 %collective-permute-done = bf16[256,2048]{1,0:T(8,128)(2,1)S(1)} collective-permute-done((bf16[256,2048]{1,0:T(8,128)(2,1)S(1)}, bf16[256,2048]{1,0:T(8,128)(2,1)S(1)}, u32[]{:S(2)}, u32[]{:S(2)}) %collective-permute-start) | collective-permute-done | bytes 1048608 | tf_op jit(solution)/shard_map/ppermute | solution.py:65
  93.9 2.1 convolution_convert_fusion.3
  96.5 2.1 convolution_convert_fusion.2
  100.1 7.1 %collective-permute-done.1 = bf16[256,1024]{1,0:T(8,128)(2,1)S(1)} collective-permute-done((bf16[256,1024]{1,0:T(8,128)(2,1)S(1)}, bf16[256,1024]{1,0:T(8,128)(2,1)S(1)}, u32[]{:S(2)}, u32[]{:S(2)}) %collective-permute-start.1) | collective-permute-done | bytes 524320 | tf_op jit(solution)/shard_map/ppermute | solution.py:71
  107.6 11.0 %collective-permute-done.2 = bf16[256,1024]{1,0:T(8,128)(2,1)} collective-permute-done((bf16[256,1024]{1,0:T(8,128)(2,1)}, bf16[256,1024]{1,0:T(8,128)(2,1)}, u32[]{:S(2)}, u32[]{:S(2)}) %collective-permute-start.2) | collective-permute-done | bytes 524320 | tf_op jit(solution)/shard_map/ppermute | solution.py:71
  120.3 7.4 %collective-permute-done.3 = bf16[256,1024]{1,0:T(8,128)(2,1)} collective-permute-done((bf16[256,1024]{1,0:T(8,128)(2,1)}, bf16[256,1024]{1,0:T(8,128)(2,1)}, u32[]{:S(2)}, u32[]{:S(2)}) %collective-permute-start.3) | collective-permute-done | bytes 524320 | tf_op jit(solution)/shard_map/ppermute | solution.py:71
  129.1 3.0 bitcast_add_fusion
  132.0 1.9 copy-done.2
  134.7 4.5 %fusion.26 = bf16[16,64,256]{2,1,0:T(8,128)(2,1)S(1)} fusion(bf16[256,16,64]{0,2,1:T(8,128)(2,1)S(1)} %bitcast.55, f32[16,256]{1,0:T(8,128)S(1)} %fusion.62, f32[16,256,256]{1,2,0:T(8,128)} %copy-done.2), kind=kOutput, calls=%fused_computation.36 | convolution fusion | flops 137629952 | bytes 5259264 | tf_op jit(solution)/shard_map/shqk,skhd->sqhd/dot_general | solution.py:93
  139.3 1.5 collective-permute-start.4
  140.8 10.3 %collective-permute-done.4 = bf16[256,1024]{0,1:T(8,128)(2,1)S(1)} collective-permute-done((bf16[256,1024]{0,1:T(8,128)(2,1)S(1)}, bf16[256,1024]{0,1:T(8,128)(2,1)S(1)}, u32[]{:S(2)}, u32[]{:S(2)}) %collective-permute-start.4) | collective-permute-done | bytes 524320 | tf_op jit(solution)/shard_map/ppermute | solution.py:97
  151.1 3.5 convolution_convert_fusion
  156.1 3.9 convolution_convert_fusion.1
  160.0 16.8 %collective-permute-done.5 = bf16[256,2048]{1,0:T(8,128)(2,1)S(1)} collective-permute-done((bf16[256,2048]{1,0:T(8,128)(2,1)S(1)}, bf16[256,2048]{1,0:T(8,128)(2,1)S(1)}, u32[]{:S(2)}, u32[]{:S(2)}) %collective-permute-start.5) | collective-permute-done | bytes 1048608 | tf_op jit(solution)/shard_map/ppermute | solution.py:101
  176.8 2.1 maximum_select_fusion
  179.1 43.6 %reduce-scatter.3.cloned.1.call-done = bf16[256,1024]{1,0:T(8,128)(2,1)} async-done(((bf16[256,4096]{1,0:T(8,128)(2,1)}), bf16[256,1024]{1,0:T(8,128)(2,1)}) %reduce-scatter.3.cloned.1.call-update) | async-done | bytes 524304 | tf_op jit(solution)/shard_map/reduce_scatter | solution.py:110
  222.7 2.0 add_convert_fusion.1
  224.8 45.0 %all-gather.6.cloned.1.call-done = bf16[256,4096]{1,0:T(8,128)(2,1)} async-done(((bf16[256,1024]{1,0:T(8,128)(2,1)}), bf16[256,4096]{1,0:T(8,128)(2,1)}) %all-gather.6.cloned.1.call-update) | async-done | bytes 2097168 | tf_op jit(solution)/shard_map/all_gather | solution.py:117
  269.8 56.9 %all-gather.8.cloned.1.call-done = bf16[512,4096]{1,0:T(8,128)(2,1)} async-done(((bf16[256,4096]{1,0:T(8,128)(2,1)}), bf16[512,4096]{1,0:T(8,128)(2,1)}) %all-gather.8.cloned.1.call-update) | async-done | bytes 4194320 | tf_op jit(solution)/shard_map/all_gather | solution.py:116
  326.7 3.2 fusion.1
  330.1 7.7 %fusion.28 = f32[512,1024]{1,0:T(8,128)S(1)} fusion(bf16[4096,1024]{1,0:T(8,128)(2,1)} %param.19, bf16[512,4096]{1,0:T(8,128)(2,1)S(1)} %copy-done.4, f32[4096]{0:T(1024)S(1)} %bitcast.57, f32[512]{0:T(512)S(1)} %add_rsqrt_fusion), kind=kOutput, calls=%fused_computation.40 | convolution fusion | flops 4303355904 | bytes 14698496 | tf_op jit(solution)/shard_map/dot_general | solution.py:120
  337.9 4.9 %fusion.25 = bf16[512,1024,1]{1,0,2:T(8,128)(2,1)S(1)} fusion(bf16[4096,1024]{1,0:T(8,128)(2,1)S(1)} %bitcast.60, f32[512,1024]{1,0:T(8,128)S(1)} %fusion.28, bf16[512,4096]{1,0:T(8,128)(2,1)S(1)} %copy-done.4, f32[4096]{0:T(1024)S(1)} %bitcast.58, f32[512]{0:T(512)S(1)} %add_rsqrt_fusion), kind=kOutput, calls=%fused_computation.35 | convolution fusion | flops 4308598784 | bytes 15747072 | tf_op jit(solution)/shard_map/dot_general | solution.py:121
  342.8 6.1 %fusion.12 = bf16[512,4,1024]{2,0,1:T(8,128)(2,1)} fusion(bf16[512,1024,1]{1,0,2:T(8,128)(2,1)S(1)} %fusion.25, bf16[128,4,8,1024]{3,2,1,0:T(8,128)(2,1)S(1)} %bitcast.63), kind=kOutput, calls=%fused_computation.21 | convolution fusion | flops 4297064448 | bytes 13631488 | tf_op jit(solution)/shard_map/tf,fmd->mtd/dot_general | solution.py:124
  349.0 88.5 %reduce-scatter.5.cloned.1.call-done = bf16[256,1024]{1,0:T(8,128)(2,1)} async-done(((bf16[2048,1024]{1,0:T(8,128)(2,1)}), bf16[256,1024]{1,0:T(8,128)(2,1)}) %reduce-scatter.5.cloned.1.call-update) | async-done | bytes 524304 | tf_op jit(solution)/shard_map/reduce_scatter | solution.py:126
  437.5 2.0 fusion.36
  (63 shorter events, 19.0 us)
Async XLA Ops:
  6.5 3.9 copy-start
  6.5 54.2 %all-gather.4.cloned.1.call-start = ((), (), s32[]{:S(2)}) async-start(), calls=%async_computation.2 | async-start | bytes 2785280 | tf_op jit(solution)/shard_map/all_gather | solution.py:59
  10.1 212.6 %reduce-scatter.3.cloned.1.call-start = ((), (), s32[]{:S(2)}) async-start(), calls=%async_computation.3 | async-start | bytes 2621440 | tf_op jit(solution)/shard_map/reduce_scatter | solution.py:110
  60.8 7.1 %copy-start.7 = (bf16[2048,1024]{1,0:T(8,128)(2,1)S(1)}, bf16[2048,1024]{1,0:T(8,128)(2,1)}, u32[]{:S(2)}) copy-start(bf16[2048,1024]{1,0:T(8,128)(2,1)} %param.13) | copy-start | bytes 12582916
  66.3 3.8 copy-start.8
  66.3 24.8 %collective-permute-start = (bf16[256,2048]{1,0:T(8,128)(2,1)S(1)}, bf16[256,2048]{1,0:T(8,128)(2,1)S(1)}, u32[]{:S(2)}, u32[]{:S(2)}) collective-permute-start(bf16[256,2048]{1,0:T(8,128)(2,1)S(1)} %constant_dynamic-slice_fusion), channel_id=1, source_target_pairs={{0,1},{1,0},{2,3},{3,2},{4,5},{5,4},{6,7},{7,6},{8,9},{9,8},{10,11... | collective-permute-start | bytes 3145736 | tf_op jit(solution)/shard_map/ppermute | solution.py:65
  70.1 2.2 copy-start.6
  92.4 14.9 %collective-permute-start.1 = (bf16[256,1024]{1,0:T(8,128)(2,1)S(1)}, bf16[256,1024]{1,0:T(8,128)(2,1)S(1)}, u32[]{:S(2)}, u32[]{:S(2)}) collective-permute-start(bf16[256,1024]{1,0:T(8,128)(2,1)S(1)} %convolution_convert_fusion.4), channel_id=1, source_target_pairs={{0,1},{1,0},{2,3},{3,2},{4,5},{5,4},{6,7},{7,6},{8,9},{9,8},{10,11... | collective-permute-start | bytes 1572872 | tf_op jit(solution)/shard_map/ppermute | solution.py:71
  96.0 22.6 %collective-permute-start.2 = (bf16[256,1024]{1,0:T(8,128)(2,1)}, bf16[256,1024]{1,0:T(8,128)(2,1)}, u32[]{:S(2)}, u32[]{:S(2)}) collective-permute-start(bf16[256,1024]{1,0:T(8,128)(2,1)} %convolution_convert_fusion.3), channel_id=1, source_target_pairs={{0,1},{1,0},{2,3},{3,2},{4,5},{5,4},{6,7},{7,6},{8,9},{9,8},{10,11... | collective-permute-start | bytes 1572872 | tf_op jit(solution)/shard_map/ppermute | solution.py:71
  98.6 29.0 %collective-permute-start.3 = (bf16[256,1024]{1,0:T(8,128)(2,1)}, bf16[256,1024]{1,0:T(8,128)(2,1)}, u32[]{:S(2)}, u32[]{:S(2)}) collective-permute-start(bf16[256,1024]{1,0:T(8,128)(2,1)} %convolution_convert_fusion.2), channel_id=1, source_target_pairs={{0,1},{1,0},{2,3},{3,2},{4,5},{5,4},{6,7},{7,6},{8,9},{9,8},{10,11... | collective-permute-start | bytes 1572872 | tf_op jit(solution)/shard_map/ppermute | solution.py:71
  132.0 2.0 copy-start.2
  139.3 11.9 %copy-start.9 = (bf16[16,64,256]{2,1,0:T(8,128)(2,1)}, bf16[16,64,256]{2,1,0:T(8,128)(2,1)S(1)}, u32[]{:S(2)}) copy-start(bf16[16,64,256]{2,1,0:T(8,128)(2,1)S(1)} %fusion.26) | copy-start | bytes 1572868
  139.3 11.9 %collective-permute-start.4 = (bf16[256,1024]{0,1:T(8,128)(2,1)S(1)}, bf16[256,1024]{0,1:T(8,128)(2,1)S(1)}, u32[]{:S(2)}, u32[]{:S(2)}) collective-permute-start(bf16[256,1024]{0,1:T(8,128)(2,1)S(1)} %bitcast.64), channel_id=1, source_target_pairs={{0,1},{1,0},{2,3},{3,2},{4,5},{5,4},{6,7},{7,6},{8,9},{9,8},{10,11... | collective-permute-start | bytes 1572872 | tf_op jit(solution)/shard_map/ppermute | solution.py:97
  154.6 22.2 %collective-permute-start.5 = (bf16[256,2048]{1,0:T(8,128)(2,1)S(1)}, bf16[256,2048]{1,0:T(8,128)(2,1)S(1)}, u32[]{:S(2)}, u32[]{:S(2)}) collective-permute-start(bf16[256,2048]{1,0:T(8,128)(2,1)S(1)} %convolution_convert_fusion), channel_id=1, source_target_pairs={{0,1},{1,0},{2,3},{3,2},{4,5},{5,4},{6,7},{7,6},{8,9},{9,8},{10,11... | collective-permute-start | bytes 3145736 | tf_op jit(solution)/shard_map/ppermute | solution.py:101
  160.0 62.7 %copy-start.5 = (bf16[1,256,1024]{2,1,0:T(8,128)(2,1)S(1)}, bf16[1,256,1024]{2,1,0:T(8,128)(2,1)}, u32[]{:S(2)}) copy-start(bf16[1,256,1024]{2,1,0:T(8,128)(2,1)} %param.11) | copy-start | bytes 1572868
  179.0 90.7 %all-gather.6.cloned.1.call-start = ((), (), s32[]{:S(2)}) async-start(), calls=%async_computation.4 | async-start | bytes 2621440 | tf_op jit(solution)/shard_map/all_gather | solution.py:117
  224.7 102.0 %all-gather.8.cloned.1.call-start = ((), (), s32[]{:S(2)}) async-start(), calls=%async_computation.5 | async-start | bytes 6291456 | tf_op jit(solution)/shard_map/all_gather | solution.py:116
  269.7 167.7 %reduce-scatter.5.cloned.1.call-start = ((), (), s32[]{:S(2)}) async-start(), calls=%async_computation.6 | async-start | bytes 4718592 | tf_op jit(solution)/shard_map/reduce_scatter | solution.py:126
  326.7 3.4 copy-start.4
  326.7 11.2 %slice-start = ((s8[8388608]{0:T(1024)(128)(4,1)}), s8[4194304]{0:T(1024)(128)(4,1)S(1)}, s32[]{:S(2)}) async-start(s8[8388608]{0:T(1024)(128)(4,1)} %bitcast.59), calls=%async_computation.7 | async-start | bytes 8388608
  326.7 16.1 %slice-start.2 = ((s8[8388608]{0:T(1024)(128)(4,1)}), s8[4194304]{0:T(1024)(128)(4,1)S(1)}, s32[]{:S(2)}) async-start(s8[8388608]{0:T(1024)(128)(4,1)} %bitcast.61), calls=%async_computation.9 | async-start | bytes 8388608
  330.1 7.8 %slice-start.1 = ((s8[8388608]{0:T(1024)(128)(4,1)}), s8[4194304]{0:T(1024)(128)(4,1)S(1)}, s32[]{:S(2)}) async-start(s8[8388608]{0:T(1024)(128)(4,1)} %bitcast.59), calls=%async_computation.8 | async-start | bytes 8388608
  330.1 12.7 %slice-start.3 = ((s8[8388608]{0:T(1024)(128)(4,1)}), s8[4194304]{0:T(1024)(128)(4,1)S(1)}, s32[]{:S(2)}) async-start(s8[8388608]{0:T(1024)(128)(4,1)} %bitcast.61), calls=%async_computation.10 | async-start | bytes 8388608
  342.8 96.7 %copy-start.1 = (f32[32,16]{0,1:T(8,128)S(1)}, f32[32,16]{0,1:T(8,128)}, u32[]{:S(2)}) copy-start(f32[32,16]{0,1:T(8,128)} %param.17) | copy-start | bytes 6148
  349.0 88.5 %copy-start.3 = (bf16[256,1024]{1,0:T(8,128)(2,1)S(1)}, bf16[256,1024]{1,0:T(8,128)(2,1)}, u32[]{:S(2)}) copy-start(bf16[256,1024]{1,0:T(8,128)(2,1)} %add_convert_fusion.1) | copy-start | bytes 1572868
Sparse Core Ops, SparseCore 0:
  10.2 50.5 all-gather.3
  179.1 43.4 reduce-scatter.2
  224.8 44.8 all-gather.5
  271.1 55.5 all-gather.7
  349.1 88.2 reduce-scatter.4

commit v2 on v1

--- a/solution.py
+++ b/solution.py
@@ -1,6 +1,10 @@
+import functools
+
 import jax
 import jax.numpy as jnp
 from jax import lax
+from jax.experimental import pallas as pl
+from jax.experimental.pallas import tpu as pltpu
 from jax.sharding import PartitionSpec as P
 
 bucket_thresholds = (1, 2, 3, 4, 5, 6, 7, 8, 11, 16, 23, 32, 45, 64, 91, 128)
@@ -25,6 +29,271 @@
     return (values * lax.rsqrt(mean_square + epsilon) * gain.astype(jnp.float32)).astype(
         jnp.bfloat16
     )
+
+
+MESH = pl.DeviceIdType.MESH
+
+
+def greet(me, count, row):
+    barrier = pltpu.get_barrier_semaphore()
+
+    @pl.when(me > 0)
+    def _():
+        pl.semaphore_signal(barrier, inc=1, device_id={"ma": me - 1}, device_id_type=MESH)
+
+    @pl.when(me < count - 1)
+    def _():
+        pl.semaphore_signal(barrier, inc=1, device_id={"ma": me + 1}, device_id_type=MESH)
+
+    pl.semaphore_signal(barrier, inc=1, device_id={"row": 1 - row}, device_id_type=MESH)
+    inner = jnp.logical_and(me > 0, me < count - 1)
+    pl.semaphore_wait(barrier, jnp.where(inner, 3, 2))
+
+
+def gather_kernel(count, pieces, x_ref, out_ref, local_sem, send_sem, z_sem, y_sem):
+    me = lax.axis_index("ma")
+    row = lax.axis_index("row")
+    length, width = x_ref.shape
+    step_rows = length // pieces
+    greet(me, count, row)
+
+    def place(block, piece, which):
+        return out_ref.at[
+            pl.ds(pl.multiple_of(which * length + piece * step_rows, step_rows), step_rows),
+            pl.ds(pl.multiple_of(block * width, width), width),
+        ]
+
+    def copy(way, block, piece, src=None):
+        here = place(block, piece, row)
+        target = ({"ma": me + 1}, {"ma": me - 1}, {"row": 1 - row})[way]
+        sem = y_sem if way == 2 else z_sem
+        return pltpu.make_async_remote_copy(
+            src_ref=here if src is None else src,
+            dst_ref=here,
+            send_sem=send_sem.at[way, block, piece],
+            recv_sem=sem.at[block, piece],
+            device_id=target,
+            device_id_type=MESH,
+        )
+
+    def own(piece):
+        return x_ref.at[pl.ds(piece * step_rows, step_rows), :]
+
+    for piece in range(pieces):
+
+        @pl.when(me < count - 1)
+        def _():
+            copy(0, me, piece, own(piece)).start()
+
+        @pl.when(me > 0)
+        def _():
+            copy(1, me, piece, own(piece)).start()
+
+        copy(2, me, piece, own(piece)).start()
+    mine = pltpu.make_async_copy(
+        x_ref,
+        out_ref.at[
+            pl.ds(pl.multiple_of(row * length, length), length),
+            pl.ds(pl.multiple_of(me * width, width), width),
+        ],
+        local_sem,
+    )
+    mine.start()
+    for step in range(1, count):
+        for piece in range(pieces):
+
+            @pl.when(me - step >= 0)
+            def _():
+                block = me - step
+                copy(0, block, piece).wait_recv()
+
+                @pl.when(me < count - 1)
+                def _():
+                    copy(0, block, piece).start()
+
+                copy(2, block, piece).start()
+
+            @pl.when(me + step < count)
+            def _():
+                block = me + step
+                copy(1, block, piece).wait_recv()
+
+                @pl.when(me > 0)
+                def _():
+                    copy(1, block, piece).start()
+
+                copy(2, block, piece).start()
+
+    mine.wait()
+    for block in range(count):
+        for piece in range(pieces):
+            here = place(block, piece, 1 - row)
+            pltpu.make_async_remote_copy(
+                src_ref=here,
+                dst_ref=here,
+                send_sem=send_sem.at[2, block, piece],
+                recv_sem=y_sem.at[block, piece],
+                device_id={"row": 1 - row},
+                device_id_type=MESH,
+            ).wait_recv()
+            copy(2, block, piece).wait_send()
+
+            @pl.when(jnp.logical_and(me < count - 1, block <= me))
+            def _():
+                copy(0, block, piece).wait_send()
+
+            @pl.when(jnp.logical_and(me > 0, block >= me))
+            def _():
+                copy(1, block, piece).wait_send()
+
+
+def gather_all(values, count, pieces, collective_id):
+    length, width = values.shape
+    return pl.pallas_call(
+        functools.partial(gather_kernel, count, pieces),
+        out_shape=jax.ShapeDtypeStruct((2 * length, count * width), values.dtype),
+        in_specs=[pl.BlockSpec(memory_space=pltpu.VMEM)],
+        out_specs=pl.BlockSpec(memory_space=pltpu.VMEM),
+        scratch_shapes=[
+            pltpu.SemaphoreType.DMA,
+            pltpu.SemaphoreType.DMA((3, count, pieces)),
+            pltpu.SemaphoreType.DMA((count, pieces)),
+            pltpu.SemaphoreType.DMA((count, pieces)),
+        ],
+        compiler_params=pltpu.CompilerParams(collective_id=collective_id, has_side_effects=True),
+    )(values)
+
+
+def reduce_kernel(
+    count, hidden_ref, down_ref, out_ref, sent, landed, total, left_in, right_in,
+    right_out, left_out, y_send, y_recv, r_send, r_recv, l_send, l_recv
+):
+    me = lax.axis_index("ma")
+    row = lax.axis_index("row")
+    length, width = out_ref.shape
+    greet(me, count, row)
+
+    def y_copy(block):
+        return pltpu.make_async_remote_copy(
+            src_ref=sent.at[block],
+            dst_ref=landed.at[block],
+            send_sem=y_send.at[block],
+            recv_sem=y_recv.at[block],
+            device_id={"row": 1 - row},
+            device_id_type=MESH,
+        )
+
+    def r_copy(block):
+        return pltpu.make_async_remote_copy(
+            src_ref=right_out.at[block],
+            dst_ref=left_in.at[block],
+            send_sem=r_send.at[block],
+            recv_sem=r_recv.at[block],
+            device_id={"ma": me + 1},
+            device_id_type=MESH,
+        )
+
+    def l_copy(block):
+        return pltpu.make_async_remote_copy(
+            src_ref=left_out.at[block],
+            dst_ref=right_in.at[block],
+            send_sem=l_send.at[block],
+            recv_sem=l_recv.at[block],
+            device_id={"ma": me - 1},
+            device_id_type=MESH,
+        )
+
+    def product(which, block):
+        rows = hidden_ref[pl.ds(pl.multiple_of(which * length, length), length), :]
+        columns = pl.ds(pl.multiple_of(block * width, width), width)
+        return jnp.dot(rows, down_ref[:, columns], preferred_element_type=jnp.float32)
+
+    def ordered(body):
+        def turn(index, carry):
+            step = count - 1 - index // 2
+            rightward = index % 2 == 0
+            block = jnp.where(rightward, me + step, me - step)
+            inside = jnp.logical_and(block >= 0, block < count)
+
+            @pl.when(jnp.logical_and(inside, jnp.logical_or(step > 0, rightward)))
+            def _():
+                body(block)
+
+            return carry
+
+        lax.fori_loop(0, 2 * count, turn, 0)
+
+    def send_peer(block):
+        sent[block] = product(1 - row, block).astype(jnp.bfloat16)
+        y_copy(block).start()
+
+    ordered(send_peer)
+
+    def pass_on(block):
+        total[...] = product(row, block)
+        y_copy(block).wait_recv()
+        total[...] = total[...] + landed[block].astype(jnp.float32)
+
+        @pl.when(jnp.logical_and(block >= me, me > 0))
+        def _():
+            r_copy(block).wait_recv()
+            total[...] = total[...] + left_in[block].astype(jnp.float32)
+
+        @pl.when(jnp.logical_and(block <= me, me < count - 1))
+        def _():
+            l_copy(block).wait_recv()
+            total[...] = total[...] + right_in[block].astype(jnp.float32)
+
+        @pl.when(block > me)
+        def _():
+            right_out[block] = total[...].astype(jnp.bfloat16)
+            r_copy(block).start()
+
+        @pl.when(block < me)
+        def _():
+            left_out[block] = total[...].astype(jnp.bfloat16)
+            l_copy(block).start()
+
+        @pl.when(block == me)
+        def _():
+            out_ref[...] = total[...]
+
+    ordered(pass_on)
+    for block in range(count):
+        y_copy(block).wait_send()
+
+        @pl.when(block > me)
+        def _():
+            r_copy(block).wait_send()
+
+        @pl.when(block < me)
+        def _():
+            l_copy(block).wait_send()
+
+
+def reduce_all(hidden, down, count, collective_id):
+    length = hidden.shape[0] // 2
+    width = down.shape[1] // count
+    blocks = pltpu.VMEM((count, length, width), jnp.bfloat16)
+    return pl.pallas_call(
+        functools.partial(reduce_kernel, count),
+        out_shape=jax.ShapeDtypeStruct((length, width), jnp.float32),
+        in_specs=[pl.BlockSpec(memory_space=pltpu.VMEM)] * 2,
+        out_specs=pl.BlockSpec(memory_space=pltpu.VMEM),
+        scratch_shapes=[
+            blocks,
+            blocks,
+            pltpu.VMEM((length, width), jnp.float32),
+            blocks,
+            blocks,
+            blocks,
+            blocks,
+        ]
+        + [pltpu.SemaphoreType.DMA((count,))] * 6,
+        compiler_params=pltpu.CompilerParams(
+            collective_id=collective_id, has_side_effects=True, vmem_limit_bytes=60 * 2**20
+        ),
+    )(hidden, down)
 
 
 def on_device(
@@ -113,19 +382,12 @@
     residual_stream = (token_float + attn_out).astype(jnp.bfloat16)
     residual_f = residual_stream.astype(jnp.float32)
     gate_full, up_full, down_full = (gate_weight, up_weight, down_projection_weight)
-    group_rows = lax.all_gather(
-        lax.all_gather(residual_stream, "ma", axis=1, tiled=True), "row", axis=0, tiled=True
-    )
+    group_rows = gather_all(residual_stream, ma_count, 2, 0)
     ffn_in = rms_scale(group_rows.astype(jnp.float32), ffn_gain_full)
     gate_act = jnp.dot(ffn_in, gate_full, preferred_element_type=jnp.float32)
     up_act = jnp.dot(ffn_in, up_full, preferred_element_type=jnp.float32)
     hidden = (jax.nn.gelu(gate_act, approximate=True) * up_act).astype(jnp.bfloat16)
-    down_blocks = down_full.reshape(down_full.shape[0], ma_count, part_width)
-    down_terms = jnp.einsum("tf,fmd->mtd", hidden, down_blocks, preferred_element_type=jnp.float32)
-    down_terms = down_terms.reshape(ma_count * ffn_in.shape[0], part_width)
-    ffn_out = lax.psum_scatter(
-        down_terms.astype(jnp.bfloat16), ("ma", "row"), scatter_dimension=0, tiled=True
-    ).astype(jnp.float32)
+    ffn_out = reduce_all(hidden, down_full, ma_count, 1)
     encoded = (residual_f + ffn_out).astype(jnp.bfloat16)
     return encoded.reshape(sequences, length, part_width)
 

time: 447 us -> 355 us (0.79)
  waiting for transfers between devices: 345 us -> 155 us
  Pallas kernels: 0 us -> 104 us
  matrix products: 47.9 us -> 42.4 us
    pallas_call x0 -> x2, Pallas kernels: none -> 104 us  [the longest x1 53.6 us: reduce_all(): pl.pallas_call(functools.partial(reduce_kernel, count), out_shape=jax.Sha...]
    all_gather x2 -> x0, waiting for transfers between devices: 102 us -> none  [the longest x1 56.9 us: on_device(): lax.all_gather(lax.all_gather(residual_stream, 'ma', axis=1, tiled=True),...]
    reduce_scatter x1 -> x0, waiting for transfers between devices: 88.5 us -> none  [on_device(): lax.psum_scatter(down_terms.astype(jnp.bfloat16), ('ma', 'row'), scatter_...]
    dot_general x1 -> x0, matrix products: 6.15 us -> none  [on_device(): jnp.einsum('tf,fmd->mtd', hidden, down_blocks, preferred_element_type=jnp...]
  transfers between devices with their start and end apart: 11 -> 8, of which waited for: 11 -> 8; matrix products, arithmetic and copies ran while one was open for 6% -> 7% of each run, Pallas kernels for 0% -> 0%
where the time goes in v2:
time: 355 us; the launch traced here: 354 us
  waiting for transfers between devices  155 us (44%)
  Pallas kernels  104 us (29%)
  matrix products  42.4 us (12%)
  other arithmetic  21 us (6%)
  between operations  13.7 us (4%)
  local copies, waits for them, and re-layouts  10.5 us (3%)
  starting transfers between devices  8.21 us (2%)
    pallas_call x1, Pallas kernels, reduce_all(): pl.pallas_call(functools.partial(reduce_kernel, count), out_shape=jax.Sha...  53.6 us
    pallas_call x1, Pallas kernels, gather_all(): pl.pallas_call(functools.partial(gather_kernel, count, pieces), out_shape...  50.4 us
    reduce_scatter x1, waiting for transfers between devices, on_device(): lax.psum_scatter(partial_out.astype(jnp.bfloat16), 'ma', scatter_dimensio...  43.6 us
    all_gather x1, waiting for transfers between devices, on_device(): lax.all_gather(jnp.concatenate([token_rows, gains]), 'ma', axis=1, tiled=...  40.8 us
    ppermute x3, waiting for transfers between devices, on_device(): incoming = [lax.ppermute(part, 'row', swap) for part in outgoing]  25.5 us
    ppermute x1, waiting for transfers between devices, on_device(): arrived = lax.ppermute(theirs, 'row', swap)  17.6 us
    ppermute x1, waiting for transfers between devices, on_device(): other_half = lax.ppermute(sent_out, 'row', swap)  16.8 us
    ppermute x1, waiting for transfers between devices, on_device(): attended_peer = lax.ppermute(attended, 'row', swap)  10.3 us
  transfers between devices with their start and end apart: 8, of which 8 were waited for; matrix products, arithmetic and copies ran while one was open for 7% of the time, Pallas kernels for 0%

profile of v2, /device:TPU:0, one launch (start us, length us, event | category | flops | bytes accessed | tf_op | source)
XLA Modules:
  0.0 354.4 jit_solution(7092361920641283248)
XLA Ops:
  8.0 2.0 maximum_maximum_fusion
  10.5 4.2 %fusion.4 = f32[256,256,16]{1,2,0:T(8,128)} fusion(s32[256,256]{1,0:T(8,128)S(1)} %fusion.31, f32[32,16]{0,1:T(8,128)S(1)} %copy-done), kind=kOutput, calls=%fused_computation.7 | convolution fusion | flops 404750336 | bytes 4458496 | tf_op jit(solution)/shard_map/dmy,du->umy/dot_general | solution.py:352
  14.6 5.3 %copy.20 = f32[256,256,16]{0,1,2:T(8,128)} copy(f32[256,256,16]{1,2,0:T(8,128)} %fusion.4) | data formatting | bytes 8388608 | tf_op jit(solution)/shard_map/dmy,du->umy/dot_general | solution.py:352
  19.9 40.8 %all-gather.2.cloned.1.call-done = bf16[272,4096]{1,0:T(8,128)(2,1)} async-done(((bf16[272,1024]{1,0:T(8,128)(2,1)}), bf16[272,4096]{1,0:T(8,128)(2,1)}) %all-gather.2.cloned.1.call-update) | async-done | bytes 2228240 | tf_op jit(solution)/shard_map/all_gather | solution.py:328
  60.7 2.2 fusion.5
  63.9 2.2 fusion.7
  66.2 1.5 collective-permute-start
  67.8 2.2 fusion.25
  73.5 17.6 %collective-permute-done = bf16[256,2048]{1,0:T(8,128)(2,1)S(1)} collective-permute-done((bf16[256,2048]{1,0:T(8,128)(2,1)S(1)}, bf16[256,2048]{1,0:T(8,128)(2,1)S(1)}, u32[]{:S(2)}, u32[]{:S(2)}) %collective-permute-start) | collective-permute-done | bytes 1048608 | tf_op jit(solution)/shard_map/ppermute | solution.py:334
  92.3 1.5 collective-permute-start.1
  93.9 2.1 convolution_convert_fusion.3
  96.5 2.1 convolution_convert_fusion.2
  100.0 7.2 %collective-permute-done.1 = bf16[256,1024]{1,0:T(8,128)(2,1)S(1)} collective-permute-done((bf16[256,1024]{1,0:T(8,128)(2,1)S(1)}, bf16[256,1024]{1,0:T(8,128)(2,1)S(1)}, u32[]{:S(2)}, u32[]{:S(2)}) %collective-permute-start.1) | collective-permute-done | bytes 524320 | tf_op jit(solution)/shard_map/ppermute | solution.py:340
  107.6 11.0 %collective-permute-done.2 = bf16[256,1024]{1,0:T(8,128)(2,1)} collective-permute-done((bf16[256,1024]{1,0:T(8,128)(2,1)}, bf16[256,1024]{1,0:T(8,128)(2,1)}, u32[]{:S(2)}, u32[]{:S(2)}) %collective-permute-start.2) | collective-permute-done | bytes 524320 | tf_op jit(solution)/shard_map/ppermute | solution.py:340
  120.2 7.4 %collective-permute-done.3 = bf16[256,1024]{1,0:T(8,128)(2,1)} collective-permute-done((bf16[256,1024]{1,0:T(8,128)(2,1)}, bf16[256,1024]{1,0:T(8,128)(2,1)}, u32[]{:S(2)}, u32[]{:S(2)}) %collective-permute-start.3) | collective-permute-done | bytes 524320 | tf_op jit(solution)/shard_map/ppermute | solution.py:340
  129.0 3.0 bitcast_add_fusion
  132.0 1.9 copy-done.3
  134.7 4.5 %fusion.19 = bf16[16,64,256]{2,1,0:T(8,128)(2,1)S(1)} fusion(bf16[256,16,64]{0,2,1:T(8,128)(2,1)S(1)} %bitcast.42, f32[16,256]{1,0:T(8,128)S(1)} %fusion.55, f32[16,256,256]{1,2,0:T(8,128)} %copy-done.3), kind=kOutput, calls=%fused_computation.31 | convolution fusion | flops 137629952 | bytes 5259264 | tf_op jit(solution)/shard_map/shqk,skhd->sqhd/dot_general | solution.py:362
  140.8 10.3 %collective-permute-done.4 = bf16[256,1024]{0,1:T(8,128)(2,1)S(1)} collective-permute-done((bf16[256,1024]{0,1:T(8,128)(2,1)S(1)}, bf16[256,1024]{0,1:T(8,128)(2,1)S(1)}, u32[]{:S(2)}, u32[]{:S(2)}) %collective-permute-start.4) | collective-permute-done | bytes 524320 | tf_op jit(solution)/shard_map/ppermute | solution.py:366
  151.1 3.5 convolution_convert_fusion
  154.6 1.5 collective-permute-start.5
  156.1 3.8 %convolution_convert_fusion.1 = bf16[256,2048]{1,0:T(8,128)(2,1)S(1)} fusion(bf16[256,1024]{0,1:T(8,128)(2,1)} %bitcast.49, bf16[1024,2048]{1,0:T(8,128)(2,1)} %param.16), kind=kOutput, calls=%fused_computation.19 | convolution fusion | flops 1074266112 | bytes 5767168 | tf_op jit(solution)/shard_map/dot_general | solution.py:371
  160.0 16.8 %collective-permute-done.5 = bf16[256,2048]{1,0:T(8,128)(2,1)S(1)} collective-permute-done((bf16[256,2048]{1,0:T(8,128)(2,1)S(1)}, bf16[256,2048]{1,0:T(8,128)(2,1)S(1)}, u32[]{:S(2)}, u32[]{:S(2)}) %collective-permute-start.5) | collective-permute-done | bytes 1048608 | tf_op jit(solution)/shard_map/ppermute | solution.py:370
  176.8 2.1 maximum_select_fusion
  179.0 43.6 %reduce-scatter.2.cloned.1.call-done = bf16[256,1024]{1,0:T(8,128)(2,1)} async-done(((bf16[256,4096]{1,0:T(8,128)(2,1)}), bf16[256,1024]{1,0:T(8,128)(2,1)}) %reduce-scatter.2.cloned.1.call-update) | async-done | bytes 524304 | tf_op jit(solution)/shard_map/reduce_scatter | solution.py:379
  222.6 2.0 add_convert_fusion.1.x_ref
  224.6 50.4 %shard_map.109 = bf16[512,4096]{1,0:T(8,128)(2,1)} custom-call(bf16[256,1024]{1,0:T(8,128)(2,1)} %add_convert_fusion.1.x_ref), custom_call_target="tpu_custom_call" | custom-call | tf_op jit(solution)/shard_map/pallas_call | solution.py:152
  275.0 3.2 fusion.1
  278.4 7.2 %fusion.21 = f32[512,1024]{1,0:T(8,128)S(1)} fusion(bf16[4096,1024]{1,0:T(8,128)(2,1)} %param.19, bf16[512,4096]{1,0:T(8,128)(2,1)S(1)} %copy-done.2, f32[4096]{0:T(1024)S(1)} %bitcast.44, f32[512]{0:T(512)S(1)} %add_rsqrt_fusion), kind=kOutput, calls=%fused_computation.35 | convolution fusion | flops 4303355904 | bytes 14698496 | tf_op jit(solution)/shard_map/dot_general | solution.py:387
  285.7 6.0 %fusion.17.hidden_ref = bf16[512,1024]{1,0:T(8,128)(2,1)} fusion(f32[512,1024]{1,0:T(8,128)S(1)} %fusion.21, bf16[4096,1024]{1,0:T(8,128)(2,1)S(1)} %bitcast.47, bf16[512,4096]{1,0:T(8,128)(2,1)S(1)} %copy-done.2, f32[4096]{0:T(1024)S(1)} %bitcast.45, f32[512]{0:T(512)S(1)} %add_rsqrt_fusion), kind=kOutput, calls=%fused_computation.28 | convolution fusion | flops 4308598784 | bytes 15747072 | tf_op jit(solution)/shard_map/dot_general | solution.py:388
  291.7 53.6 %shard_map.110 = f32[256,1024]{1,0:T(8,128)} custom-call(bf16[512,1024]{1,0:T(8,128)(2,1)} %fusion.17.hidden_ref, bf16[1024,4096]{1,0:T(8,128)(2,1)} %down_ref.1), custom_call_target="tpu_custom_call" | custom-call | tf_op jit(solution)/shard_map/pallas_call | solution.py:278
  345.4 2.2 fusion.29
  (50 shorter events, 15.7 us)
Async XLA Ops:
  6.5 3.9 %copy-start = (f32[32,16]{0,1:T(8,128)S(1)}, f32[32,16]{0,1:T(8,128)}, u32[]{:S(2)}) copy-start(f32[32,16]{0,1:T(8,128)} %param.17) | copy-start | bytes 6148
  6.5 54.2 %all-gather.2.cloned.1.call-start = ((), (), s32[]{:S(2)}) async-start(), calls=%async_computation.1 | async-start | bytes 2785280 | tf_op jit(solution)/shard_map/all_gather | solution.py:328
  10.0 212.6 %reduce-scatter.2.cloned.1.call-start = ((), (), s32[]{:S(2)}) async-start(), calls=%async_computation.2 | async-start | bytes 2621440 | tf_op jit(solution)/shard_map/reduce_scatter | solution.py:379
  60.7 7.1 %copy-start.7 = (bf16[2048,1024]{1,0:T(8,128)(2,1)S(1)}, bf16[2048,1024]{1,0:T(8,128)(2,1)}, u32[]{:S(2)}) copy-start(bf16[2048,1024]{1,0:T(8,128)(2,1)} %param.13) | copy-start | bytes 12582916
  66.2 3.8 %copy-start.8 = (bf16[2048,1024]{1,0:T(8,128)(2,1)S(1)}, bf16[2048,1024]{1,0:T(8,128)(2,1)}, u32[]{:S(2)}) copy-start(bf16[2048,1024]{1,0:T(8,128)(2,1)} %param.14) | copy-start | bytes 12582916
  66.2 24.8 %collective-permute-start = (bf16[256,2048]{1,0:T(8,128)(2,1)S(1)}, bf16[256,2048]{1,0:T(8,128)(2,1)S(1)}, u32[]{:S(2)}, u32[]{:S(2)}) collective-permute-start(bf16[256,2048]{1,0:T(8,128)(2,1)S(1)} %constant_dynamic-slice_fusion), channel_id=1, source_target_pairs={{0,1},{1,0},{2,3},{3,2},{4,5},{5,4},{6,7},{7,6},{8,9},{9,8},{10,11... | collective-permute-start | bytes 3145736 | tf_op jit(solution)/shard_map/ppermute | solution.py:334
  70.0 2.2 copy-start.6
  92.3 14.9 %collective-permute-start.1 = (bf16[256,1024]{1,0:T(8,128)(2,1)S(1)}, bf16[256,1024]{1,0:T(8,128)(2,1)S(1)}, u32[]{:S(2)}, u32[]{:S(2)}) collective-permute-start(bf16[256,1024]{1,0:T(8,128)(2,1)S(1)} %convolution_convert_fusion.4), channel_id=1, source_target_pairs={{0,1},{1,0},{2,3},{3,2},{4,5},{5,4},{6,7},{7,6},{8,9},{9,8},{10,11... | collective-permute-start | bytes 1572872 | tf_op jit(solution)/shard_map/ppermute | solution.py:340
  95.9 22.6 %collective-permute-start.2 = (bf16[256,1024]{1,0:T(8,128)(2,1)}, bf16[256,1024]{1,0:T(8,128)(2,1)}, u32[]{:S(2)}, u32[]{:S(2)}) collective-permute-start(bf16[256,1024]{1,0:T(8,128)(2,1)} %convolution_convert_fusion.3), channel_id=1, source_target_pairs={{0,1},{1,0},{2,3},{3,2},{4,5},{5,4},{6,7},{7,6},{8,9},{9,8},{10,11... | collective-permute-start | bytes 1572872 | tf_op jit(solution)/shard_map/ppermute | solution.py:340
  98.5 29.1 %collective-permute-start.3 = (bf16[256,1024]{1,0:T(8,128)(2,1)}, bf16[256,1024]{1,0:T(8,128)(2,1)}, u32[]{:S(2)}, u32[]{:S(2)}) collective-permute-start(bf16[256,1024]{1,0:T(8,128)(2,1)} %convolution_convert_fusion.2), channel_id=1, source_target_pairs={{0,1},{1,0},{2,3},{3,2},{4,5},{5,4},{6,7},{7,6},{8,9},{9,8},{10,11... | collective-permute-start | bytes 1572872 | tf_op jit(solution)/shard_map/ppermute | solution.py:340
  132.0 1.9 copy-start.3
  139.3 11.9 %copy-start.9 = (bf16[16,64,256]{2,1,0:T(8,128)(2,1)}, bf16[16,64,256]{2,1,0:T(8,128)(2,1)S(1)}, u32[]{:S(2)}) copy-start(bf16[16,64,256]{2,1,0:T(8,128)(2,1)S(1)} %fusion.19) | copy-start | bytes 1572868
  139.3 11.9 %collective-permute-start.4 = (bf16[256,1024]{0,1:T(8,128)(2,1)S(1)}, bf16[256,1024]{0,1:T(8,128)(2,1)S(1)}, u32[]{:S(2)}, u32[]{:S(2)}) collective-permute-start(bf16[256,1024]{0,1:T(8,128)(2,1)S(1)} %bitcast.48), channel_id=1, source_target_pairs={{0,1},{1,0},{2,3},{3,2},{4,5},{5,4},{6,7},{7,6},{8,9},{9,8},{10,11... | collective-permute-start | bytes 1572872 | tf_op jit(solution)/shard_map/ppermute | solution.py:366
  154.6 22.2 %collective-permute-start.5 = (bf16[256,2048]{1,0:T(8,128)(2,1)S(1)}, bf16[256,2048]{1,0:T(8,128)(2,1)S(1)}, u32[]{:S(2)}, u32[]{:S(2)}) collective-permute-start(bf16[256,2048]{1,0:T(8,128)(2,1)S(1)} %convolution_convert_fusion), channel_id=1, source_target_pairs={{0,1},{1,0},{2,3},{3,2},{4,5},{5,4},{6,7},{7,6},{8,9},{9,8},{10,11... | collective-permute-start | bytes 3145736 | tf_op jit(solution)/shard_map/ppermute | solution.py:370
  160.0 62.6 %copy-start.5 = (bf16[1,256,1024]{2,1,0:T(8,128)(2,1)S(1)}, bf16[1,256,1024]{2,1,0:T(8,128)(2,1)}, u32[]{:S(2)}) copy-start(bf16[1,256,1024]{2,1,0:T(8,128)(2,1)} %param.11) | copy-start | bytes 1572868
  275.0 3.5 copy-start.2
  275.0 10.7 %slice-start = ((s8[8388608]{0:T(1024)(128)(4,1)}), s8[4194304]{0:T(1024)(128)(4,1)S(1)}, s32[]{:S(2)}) async-start(s8[8388608]{0:T(1024)(128)(4,1)} %bitcast.46), calls=%async_computation.3 | async-start | bytes 8388608
  278.4 7.2 %slice-start.1 = ((s8[8388608]{0:T(1024)(128)(4,1)}), s8[4194304]{0:T(1024)(128)(4,1)S(1)}, s32[]{:S(2)}) async-start(s8[8388608]{0:T(1024)(128)(4,1)} %bitcast.46), calls=%async_computation.4 | async-start | bytes 8388608
  285.7 61.9 %copy-start.1 = (f32[32,16]{0,1:T(8,128)S(1)}, f32[32,16]{0,1:T(8,128)}, u32[]{:S(2)}) copy-start(f32[32,16]{0,1:T(8,128)} %param.17) | copy-start | bytes 6148
  291.7 53.7 %copy-start.4 = (bf16[256,1024]{1,0:T(8,128)(2,1)S(1)}, bf16[256,1024]{1,0:T(8,128)(2,1)}, u32[]{:S(2)}) copy-start(bf16[256,1024]{1,0:T(8,128)(2,1)} %add_convert_fusion.1.x_ref) | copy-start | bytes 1572868
Sparse Core Ops, SparseCore 0:
  10.2 50.5 all-gather.1
  179.1 43.4 reduce-scatter.1

commit v3 on v2

--- a/solution.py
+++ b/solution.py
@@ -164,136 +164,148 @@
     )(values)
 
 
-def reduce_kernel(
-    count, hidden_ref, down_ref, out_ref, sent, landed, total, left_in, right_in,
-    right_out, left_out, y_send, y_recv, r_send, r_recv, l_send, l_recv
-):
+def reduce_kernel(count, pieces, paired, left_ref, right_ref, out_ref, *scratch):
+    if paired:
+        sent, landed, y_send, y_recv = scratch[:4]
+    total, left_in, right_in, right_out, left_out, r_send, r_recv, l_send, l_recv = scratch[-9:]
     me = lax.axis_index("ma")
     row = lax.axis_index("row")
     length, width = out_ref.shape
+    step_rows = length // pieces
     greet(me, count, row)
 
-    def y_copy(block):
+    def y_copy(unit):
         return pltpu.make_async_remote_copy(
-            src_ref=sent.at[block],
-            dst_ref=landed.at[block],
-            send_sem=y_send.at[block],
-            recv_sem=y_recv.at[block],
+            src_ref=sent.at[unit],
+            dst_ref=landed.at[unit],
+            send_sem=y_send.at[unit],
+            recv_sem=y_recv.at[unit],
             device_id={"row": 1 - row},
             device_id_type=MESH,
         )
 
-    def r_copy(block):
+    def r_copy(unit):
         return pltpu.make_async_remote_copy(
-            src_ref=right_out.at[block],
-            dst_ref=left_in.at[block],
-            send_sem=r_send.at[block],
-            recv_sem=r_recv.at[block],
+            src_ref=right_out.at[unit],
+            dst_ref=left_in.at[unit],
+            send_sem=r_send.at[unit],
+            recv_sem=r_recv.at[unit],
             device_id={"ma": me + 1},
             device_id_type=MESH,
         )
 
-    def l_copy(block):
+    def l_copy(unit):
         return pltpu.make_async_remote_copy(
-            src_ref=left_out.at[block],
-            dst_ref=right_in.at[block],
-            send_sem=l_send.at[block],
-            recv_sem=l_recv.at[block],
+            src_ref=left_out.at[unit],
+            dst_ref=right_in.at[unit],
+            send_sem=l_send.at[unit],
+            recv_sem=l_recv.at[unit],
             device_id={"ma": me - 1},
             device_id_type=MESH,
         )
 
-    def product(which, block):
-        rows = hidden_ref[pl.ds(pl.multiple_of(which * length, length), length), :]
+    def product(which, block, piece):
+        start = pl.multiple_of(which * length + piece * step_rows, step_rows)
         columns = pl.ds(pl.multiple_of(block * width, width), width)
-        return jnp.dot(rows, down_ref[:, columns], preferred_element_type=jnp.float32)
+        return jnp.dot(
+            left_ref[pl.ds(start, step_rows), :],
+            right_ref[:, columns],
+            preferred_element_type=jnp.float32,
+        )
 
     def ordered(body):
         def turn(index, carry):
-            step = count - 1 - index // 2
-            rightward = index % 2 == 0
+            piece = index % pieces
+            side = index // pieces
+            step = count - 1 - side // 2
+            rightward = side % 2 == 0
             block = jnp.where(rightward, me + step, me - step)
             inside = jnp.logical_and(block >= 0, block < count)
 
             @pl.when(jnp.logical_and(inside, jnp.logical_or(step > 0, rightward)))
             def _():
-                body(block)
+                body(block, piece, block * pieces + piece)
 
             return carry
 
-        lax.fori_loop(0, 2 * count, turn, 0)
-
-    def send_peer(block):
-        sent[block] = product(1 - row, block).astype(jnp.bfloat16)
-        y_copy(block).start()
-
-    ordered(send_peer)
-
-    def pass_on(block):
-        total[...] = product(row, block)
-        y_copy(block).wait_recv()
-        total[...] = total[...] + landed[block].astype(jnp.float32)
+        lax.fori_loop(0, 2 * count * pieces, turn, 0)
+
+    def send_peer(block, piece, unit):
+        sent[unit] = product(1 - row, block, piece).astype(jnp.bfloat16)
+        y_copy(unit).start()
+
+    if paired:
+        ordered(send_peer)
+
+    def pass_on(block, piece, unit):
+        total[...] = product(row if paired else 0, block, piece)
+        if paired:
+            y_copy(unit).wait_recv()
+            total[...] = total[...] + landed[unit].astype(jnp.float32)
 
         @pl.when(jnp.logical_and(block >= me, me > 0))
         def _():
-            r_copy(block).wait_recv()
-            total[...] = total[...] + left_in[block].astype(jnp.float32)
+            r_copy(unit).wait_recv()
+            total[...] = total[...] + left_in[unit].astype(jnp.float32)
 
         @pl.when(jnp.logical_and(block <= me, me < count - 1))
         def _():
-            l_copy(block).wait_recv()
-            total[...] = total[...] + right_in[block].astype(jnp.float32)
+            l_copy(unit).wait_recv()
+            total[...] = total[...] + right_in[unit].astype(jnp.float32)
 
         @pl.when(block > me)
         def _():
-            right_out[block] = total[...].astype(jnp.bfloat16)
-            r_copy(block).start()
+            right_out[unit] = total[...].astype(jnp.bfloat16)
+            r_copy(unit).start()
 
         @pl.when(block < me)
         def _():
-            left_out[block] = total[...].astype(jnp.bfloat16)
-            l_copy(block).start()
+            left_out[unit] = total[...].astype(jnp.bfloat16)
+            l_copy(unit).start()
 
         @pl.when(block == me)
         def _():
-            out_ref[...] = total[...]
+            out_ref[pl.ds(pl.multiple_of(piece * step_rows, step_rows), step_rows), :] = total[...]
 
     ordered(pass_on)
-    for block in range(count):
-        y_copy(block).wait_send()
+
+    def drain(unit, carry):
+        block = unit // pieces
+        if paired:
+            y_copy(unit).wait_send()
 
         @pl.when(block > me)
         def _():
-            r_copy(block).wait_send()
+            r_copy(unit).wait_send()
 
         @pl.when(block < me)
         def _():
-            l_copy(block).wait_send()
-
-
-def reduce_all(hidden, down, count, collective_id):
-    length = hidden.shape[0] // 2
-    width = down.shape[1] // count
-    blocks = pltpu.VMEM((count, length, width), jnp.bfloat16)
+            l_copy(unit).wait_send()
+
+        return carry
+
+    lax.fori_loop(0, count * pieces, drain, 0)
+
+
+def reduce_all(left, right, count, pieces, paired, collective_id):
+    length = left.shape[0] // (2 if paired else 1)
+    width = right.shape[1] // count
+    units = count * pieces
+    blocks = pltpu.VMEM((units, length // pieces, width), jnp.bfloat16)
+    sems = pltpu.SemaphoreType.DMA((units,))
     return pl.pallas_call(
-        functools.partial(reduce_kernel, count),
+        functools.partial(reduce_kernel, count, pieces, paired),
         out_shape=jax.ShapeDtypeStruct((length, width), jnp.float32),
         in_specs=[pl.BlockSpec(memory_space=pltpu.VMEM)] * 2,
         out_specs=pl.BlockSpec(memory_space=pltpu.VMEM),
-        scratch_shapes=[
-            blocks,
-            blocks,
-            pltpu.VMEM((length, width), jnp.float32),
-            blocks,
-            blocks,
-            blocks,
-            blocks,
-        ]
-        + [pltpu.SemaphoreType.DMA((count,))] * 6,
+        scratch_shapes=([blocks, blocks, sems, sems] if paired else [])
+        + [pltpu.VMEM((length // pieces, width), jnp.float32)]
+        + [blocks] * 4
+        + [sems] * 4,
         compiler_params=pltpu.CompilerParams(
             collective_id=collective_id, has_side_effects=True, vmem_limit_bytes=60 * 2**20
         ),
-    )(hidden, down)
+    )(left, right)
 
 
 def on_device(
@@ -321,6 +333,12 @@
     half = query_weight.shape[0]
     swap = [(i, i ^ 1) for i in range(row_count)]
     my_row = lax.axis_index("row")
+    ba_count = lax.axis_size("ba")
+    lane = lax.axis_index("ba") % 2
+    half_rows = attention_output_matrix.shape[0] // 2
+    out_piece = lax.dynamic_slice_in_dim(attention_output_matrix, lane * half_rows, half_rows, 0)
+    out_other = lax.ppermute(out_piece, "row", swap)
+    out_rest = lax.ppermute(out_other, "ba", [(i, i ^ 1) for i in range(ba_count)])
     gains = jnp.concatenate(
         [attn_gain.reshape(1, part_width), ffn_gain.reshape(1, part_width)]
         + [jnp.zeros((14, part_width), jnp.bfloat16)]
@@ -363,22 +381,17 @@
         "shqk,skhd->sqhd", weights, value_heads, preferred_element_type=jnp.float32
     )
     attended = attended.astype(jnp.bfloat16).reshape(slab_rows, inner_width)
-    attended_peer = lax.ppermute(attended, "row", swap)
-    sent_out = jnp.dot(
-        attended_peer, attention_output_matrix, preferred_element_type=jnp.float32
-    ).astype(jnp.bfloat16)
-    other_half = lax.ppermute(sent_out, "row", swap)
-    own_half = jnp.dot(
-        attended, attention_output_matrix, preferred_element_type=jnp.float32
-    ).astype(jnp.bfloat16)
-    partial_out = jnp.where(
+    out_far = jnp.where(
+        lane == 0,
+        jnp.concatenate([out_other, out_rest]),
+        jnp.concatenate([out_rest, out_other]),
+    )
+    out_full = jnp.where(
         my_row == 0,
-        jnp.concatenate([own_half, other_half], axis=1),
-        jnp.concatenate([other_half, own_half], axis=1),
-    )
-    attn_out = lax.psum_scatter(
-        partial_out.astype(jnp.bfloat16), "ma", scatter_dimension=1, tiled=True
-    ).astype(jnp.float32)
+        jnp.concatenate([attention_output_matrix, out_far], axis=1),
+        jnp.concatenate([out_far, attention_output_matrix], axis=1),
+    )
+    attn_out = reduce_all(attended, out_full, ma_count, 2, False, 2)
     residual_stream = (token_float + attn_out).astype(jnp.bfloat16)
     residual_f = residual_stream.astype(jnp.float32)
     gate_full, up_full, down_full = (gate_weight, up_weight, down_projection_weight)
@@ -387,7 +400,7 @@
     gate_act = jnp.dot(ffn_in, gate_full, preferred_element_type=jnp.float32)
     up_act = jnp.dot(ffn_in, up_full, preferred_element_type=jnp.float32)
     hidden = (jax.nn.gelu(gate_act, approximate=True) * up_act).astype(jnp.bfloat16)
-    ffn_out = reduce_all(hidden, down_full, ma_count, 1)
+    ffn_out = reduce_all(hidden, down_full, ma_count, 2, True, 1)
     encoded = (residual_f + ffn_out).astype(jnp.bfloat16)
     return encoded.reshape(sequences, length, part_width)
 

time: 355 us -> 306 us (0.86)
  waiting for transfers between devices: 155 us -> 65.5 us
  Pallas kernels: 104 us -> 143 us
  matrix products: 42.4 us -> 35.3 us
  other arithmetic: 21 us -> 27.6 us
    reduce_scatter x1 -> x0, waiting for transfers between devices: 43.6 us -> none  [on_device(): lax.psum_scatter(partial_out.astype(jnp.bfloat16), 'ma', scatter_dimensio...]
    all_gather x1, waiting for transfers between devices: 40.8 us -> 0.15 us  [on_device(): lax.all_gather(jnp.concatenate([token_rows, gains]), 'ma', axis=1, tiled=...]
    pallas_call x1 -> x2, Pallas kernels: 53.6 us -> 93.6 us  [reduce_all(): pl.pallas_call(functools.partial(reduce_kernel, count, pieces, paired), o...]
    ppermute x2, waiting for transfers between devices: 27.2 us -> 35.8 us  [the longest x1 35.8 us: on_device(): out_other = lax.ppermute(out_piece, 'row', swap)]
    ppermute x1, waiting for transfers between devices: 17.6 us -> 9.25 us  [on_device(): arrived = lax.ppermute(theirs, 'row', swap)]
    select_n x1 -> x2, other arithmetic: 2.15 us -> 9.61 us  [the longest x1 5.55 us: on_device(): jnp.where(my_row == 0, jnp.concatenate([attention_output_matrix, out_far]...]
    dot_general x2 -> x0, matrix products: 7.3 us -> none  [the longest x1 3.85 us: on_device(): jnp.dot(attended, attention_output_matrix, preferred_element_type=jnp.flo...]
    ppermute x3, waiting for transfers between devices: 25.5 us -> 20.3 us  [on_device(): incoming = [lax.ppermute(part, 'row', swap) for part in outgoing]]
  transfers between devices with their start and end apart: 8 -> 7, of which waited for: 8 -> 6; matrix products, arithmetic and copies ran while one was open for 7% -> 14% of each run, Pallas kernels for 0% -> 0%
where the time goes in v3:
time: 306 us
  Pallas kernels  143 us (47%)
  waiting for transfers between devices  65.5 us (21%)
  matrix products  35.3 us (12%)
  other arithmetic  27.6 us (9%)
  between operations  13.7 us (4%)
  local copies, waits for them, and re-layouts  12.5 us (4%)
  starting transfers between devices  8.56 us (3%)
    pallas_call x2, Pallas kernels, reduce_all(): pl.pallas_call(functools.partial(reduce_kernel, count, pieces, paired), o...  93.6 us
    pallas_call x1, Pallas kernels, gather_all(): pl.pallas_call(functools.partial(gather_kernel, count, pieces), out_shape...  48.9 us
    ppermute x1, waiting for transfers between devices, on_device(): out_other = lax.ppermute(out_piece, 'row', swap)  35.8 us
    ppermute x3, waiting for transfers between devices, on_device(): incoming = [lax.ppermute(part, 'row', swap) for part in outgoing]  20.3 us
    ppermute x1, waiting for transfers between devices, on_device(): arrived = lax.ppermute(theirs, 'row', swap)  9.25 us
    dot_general x1, matrix products, on_device(): gate_act = jnp.dot(ffn_in, gate_full, preferred_element_type=jnp.float32)  7.32 us
  transfers between devices with their start and end apart: 7, of which 6 were waited for; matrix products, arithmetic and copies ran while one was open for 14% of the time, Pallas kernels for 0%

profile of v3, /device:TPU:0, one launch (start us, length us, event | category | flops | bytes accessed | tf_op | source)
XLA Modules:
  0.0 305.6 jit_solution(3629382620780409588)
XLA Ops:
  8.0 2.1 maximum_maximum_fusion
  10.1 1.7 constant_dynamic-slice_fusion
  11.8 3.1 %collective-permute-start.4 = (bf16[512,2048]{1,0:T(8,128)(2,1)S(1)}, bf16[512,2048]{1,0:T(8,128)(2,1)}, u32[]{:S(2)}, u32[]{:S(2)}) collective-permute-start(bf16[512,2048]{1,0:T(8,128)(2,1)S(1)} %constant_dynamic-slice_fusion), channel_id=1, source_target_pairs={{0,1},{1,0},{2,3},{3,2},{4,5},{5,4},{6,7},{7,6},{8,9},{9,8},{10,11... | collective-permute-start | bytes 6291464 | tf_op jit(solution)/shard_map/ppermute | solution.py:340
  15.3 4.2 %fusion.4 = f32[256,256,16]{1,2,0:T(8,128)} fusion(s32[256,256]{1,0:T(8,128)S(1)} %fusion.31, f32[32,16]{0,1:T(8,128)S(1)} %copy-done), kind=kOutput, calls=%fused_computation.8 | convolution fusion | flops 404750336 | bytes 4458496 | tf_op jit(solution)/shard_map/dmy,du->umy/dot_general | solution.py:370
  19.4 5.4 %copy.21 = f32[256,256,16]{0,1,2:T(8,128)} copy(f32[256,256,16]{1,2,0:T(8,128)} %fusion.4) | data formatting | bytes 8388608 | tf_op jit(solution)/shard_map/dmy,du->umy/dot_general | solution.py:370
  24.8 35.8 %collective-permute-done.4 = bf16[512,2048]{1,0:T(8,128)(2,1)} collective-permute-done((bf16[512,2048]{1,0:T(8,128)(2,1)S(1)}, bf16[512,2048]{1,0:T(8,128)(2,1)}, u32[]{:S(2)}, u32[]{:S(2)}) %collective-permute-start.4) | collective-permute-done | bytes 2097184 | tf_op jit(solution)/shard_map/ppermute | solution.py:340
  60.8 2.2 fusion.5
  64.0 2.2 fusion.7
  66.3 1.7 collective-permute-start
  69.3 2.3 fusion.23
  72.9 4.1 %maximum_select_fusion.1 = bf16[1024,2048]{1,0:T(8,128)(2,1)S(1)} fusion(bf16[512,2048]{1,0:T(8,128)(2,1)S(1)} %collective-permute-done.5, bf16[512,2048]{1,0:T(8,128)(2,1)} %collective-permute-done.4, pred[]{:T(512)S(6)} %eq.25), kind=kLoop, calls=%fused_computation.14 | loop fusion | flops 18874368 | bytes 8388609 | tf_op jit(solution)/shard_map/jit(_where)/select_n | solution.py:384
  77.0 5.6 %maximum_select_fusion.right_ref = bf16[1024,4096]{1,0:T(8,128)(2,1)} fusion(bf16[1024,2048]{1,0:T(8,128)(2,1)S(1)} %maximum_select_fusion.1, bf16[1024,2048]{1,0:T(8,128)(2,1)S(1)} %copy-done.4, pred[]{:T(512)S(6)} %eq.24), kind=kLoop, calls=%fused_computation.6 | loop fusion | flops 37748736 | bytes 16777216 | tf_op jit(solution)/shard_map/jit(_where)/select_n | solution.py:389
  82.5 9.3 %collective-permute-done = bf16[256,2048]{1,0:T(8,128)(2,1)S(1)} collective-permute-done((bf16[256,2048]{1,0:T(8,128)(2,1)S(1)}, bf16[256,2048]{1,0:T(8,128)(2,1)S(1)}, u32[]{:S(2)}, u32[]{:S(2)}) %collective-permute-start) | collective-permute-done | bytes 1048608 | tf_op jit(solution)/shard_map/ppermute | solution.py:352
  93.1 1.8 collective-permute-start.2
  94.9 2.1 convolution_convert_fusion
  97.2 2.1 convolution_convert_fusion.2
  99.3 1.7 collective-permute-start.1
  101.0 6.9 %collective-permute-done.2 = bf16[256,1024]{1,0:T(8,128)(2,1)S(1)} collective-permute-done((bf16[256,1024]{1,0:T(8,128)(2,1)S(1)}, bf16[256,1024]{1,0:T(8,128)(2,1)S(1)}, u32[]{:S(2)}, u32[]{:S(2)}) %collective-permute-start.2) | collective-permute-done | bytes 524320 | tf_op jit(solution)/shard_map/ppermute | solution.py:358
  108.3 11.0 %collective-permute-done.3 = bf16[256,1024]{1,0:T(8,128)(2,1)} collective-permute-done((bf16[256,1024]{1,0:T(8,128)(2,1)}, bf16[256,1024]{1,0:T(8,128)(2,1)}, u32[]{:S(2)}, u32[]{:S(2)}) %collective-permute-start.3) | collective-permute-done | bytes 524320 | tf_op jit(solution)/shard_map/ppermute | solution.py:358
  119.3 1.5 add_convert_fusion.2
  121.0 3.0 bitcast_add_fusion
  124.0 1.9 copy-done.2
  126.7 2.4 collective-permute-done.1
  129.4 4.5 %fusion.19 = bf16[16,64,256]{2,1,0:T(8,128)(2,1)S(1)} fusion(bf16[256,16,64]{0,2,1:T(8,128)(2,1)S(1)} %bitcast.38, f32[16,256]{1,0:T(8,128)S(1)} %fusion.55, f32[16,256,256]{1,2,0:T(8,128)} %copy-done.2), kind=kOutput, calls=%fused_computation.30 | convolution fusion | flops 137629952 | bytes 5259264 | tf_op jit(solution)/shard_map/shqk,skhd->sqhd/dot_general | solution.py:380
  135.0 42.0 %shard_map.109 = f32[256,1024]{1,0:T(8,128)} custom-call(bf16[256,1024]{1,0:T(8,128)(2,1)} %copy.23.left_ref, bf16[1024,4096]{1,0:T(8,128)(2,1)} %maximum_select_fusion.right_ref), custom_call_target="tpu_custom_call" | custom-call | tf_op jit(solution)/shard_map/pallas_call | solution.py:296
  177.0 2.2 add_convert_fusion.1.x_ref
  179.2 48.9 %shard_map.110 = bf16[512,4096]{1,0:T(8,128)(2,1)} custom-call(bf16[256,1024]{1,0:T(8,128)(2,1)} %add_convert_fusion.1.x_ref), custom_call_target="tpu_custom_call" | custom-call | tf_op jit(solution)/shard_map/pallas_call | solution.py:152
  228.1 3.2 %fusion.1 = f32[512]{0:T(512)S(1)} fusion(bf16[512,4096]{1,0:T(8,128)(2,1)} %shard_map.110), kind=kLoop, calls=%fused_computation.3 | loop fusion | flops 6290944 | bytes 4196352 | tf_op jit(solution)/shard_map/reduce_sum | solution.py:28
  231.5 7.3 %fusion.21 = f32[512,1024]{1,0:T(8,128)S(1)} fusion(bf16[4096,1024]{1,0:T(8,128)(2,1)} %param.19, bf16[512,4096]{1,0:T(8,128)(2,1)S(1)} %copy-done.3, f32[4096]{0:T(1024)S(1)} %bitcast.41, f32[512]{0:T(512)S(1)} %add_rsqrt_fusion), kind=kOutput, calls=%fused_computation.34 | convolution fusion | flops 4303355904 | bytes 14698496 | tf_op jit(solution)/shard_map/dot_general | solution.py:400
  238.9 6.0 %fusion.17.left_ref = bf16[512,1024]{1,0:T(8,128)(2,1)} fusion(f32[512,1024]{1,0:T(8,128)S(1)} %fusion.21, bf16[4096,1024]{1,0:T(8,128)(2,1)S(1)} %bitcast.44, bf16[512,4096]{1,0:T(8,128)(2,1)S(1)} %copy-done.3, f32[4096]{0:T(1024)S(1)} %bitcast.42, f32[512]{0:T(512)S(1)} %add_rsqrt_fusion), kind=kOutput, calls=%fused_computation.28 | convolution fusion | flops 4308598784 | bytes 15747072 | tf_op jit(solution)/shard_map/dot_general | solution.py:401
  244.9 51.7 %shard_map.111 = f32[256,1024]{1,0:T(8,128)} custom-call(bf16[512,1024]{1,0:T(8,128)(2,1)} %fusion.17.left_ref, bf16[1024,4096]{1,0:T(8,128)(2,1)} %right_ref.1), custom_call_target="tpu_custom_call" | custom-call | tf_op jit(solution)/shard_map/pallas_call | solution.py:296
  296.6 2.2 fusion.29
  (49 shorter events, 10.1 us)
Async XLA Ops:
  6.5 8.7 %copy-start = (f32[32,16]{0,1:T(8,128)S(1)}, f32[32,16]{0,1:T(8,128)}, u32[]{:S(2)}) copy-start(f32[32,16]{0,1:T(8,128)} %param.17) | copy-start | bytes 6148
  6.5 54.2 %all-gather.2.cloned.1.call-start = ((), (), s32[]{:S(2)}) async-start(), calls=%async_computation | async-start | bytes 2785280 | tf_op jit(solution)/shard_map/all_gather | solution.py:346
  11.8 48.8 %collective-permute-start.4 = (bf16[512,2048]{1,0:T(8,128)(2,1)S(1)}, bf16[512,2048]{1,0:T(8,128)(2,1)}, u32[]{:S(2)}, u32[]{:S(2)}) collective-permute-start(bf16[512,2048]{1,0:T(8,128)(2,1)S(1)} %constant_dynamic-slice_fusion), channel_id=1, source_target_pairs={{0,1},{1,0},{2,3},{3,2},{4,5},{5,4},{6,7},{7,6},{8,9},{9,8},{10,11... | collective-permute-start | bytes 6291464 | tf_op jit(solution)/shard_map/ppermute | solution.py:340
  60.6 12.3 %collective-permute-start.5 = (bf16[512,2048]{1,0:T(8,128)(2,1)}, bf16[512,2048]{1,0:T(8,128)(2,1)S(1)}, u32[]{:S(2)}, u32[]{:S(2)}) collective-permute-start(bf16[512,2048]{1,0:T(8,128)(2,1)} %collective-permute-done.4), channel_id=1, source_target_pairs={{0,8},{8,0},{16,24},{24,16},{1,9},{9,1},{17,25},{25,17},{2,10},{10... | collective-permute-start | bytes 6291464 | tf_op jit(solution)/shard_map/ppermute | solution.py:341
  60.8 7.2 %copy-start.7 = (bf16[2048,1024]{1,0:T(8,128)(2,1)S(1)}, bf16[2048,1024]{1,0:T(8,128)(2,1)}, u32[]{:S(2)}) copy-start(bf16[2048,1024]{1,0:T(8,128)(2,1)} %param.13) | copy-start | bytes 12582916
  66.3 3.0 copy-start.8
  66.3 25.5 %collective-permute-start = (bf16[256,2048]{1,0:T(8,128)(2,1)S(1)}, bf16[256,2048]{1,0:T(8,128)(2,1)S(1)}, u32[]{:S(2)}, u32[]{:S(2)}) collective-permute-start(bf16[256,2048]{1,0:T(8,128)(2,1)S(1)} %constant_dynamic-slice_fusion.1), channel_id=1, source_target_pairs={{0,1},{1,0},{2,3},{3,2},{4,5},{5,4},{6,7},{7,6},{8,9},{9,8},{10,11... | collective-permute-start | bytes 3145736 | tf_op jit(solution)/shard_map/ppermute | solution.py:352
  69.3 2.3 copy-start.9
  72.9 4.1 %copy-start.4 = (bf16[1024,2048]{1,0:T(8,128)(2,1)S(1)}, bf16[1024,2048]{1,0:T(8,128)(2,1)}, u32[]{:S(2)}) copy-start(bf16[1024,2048]{1,0:T(8,128)(2,1)} %param.16) | copy-start | bytes 12582916
  93.1 14.9 %collective-permute-start.2 = (bf16[256,1024]{1,0:T(8,128)(2,1)S(1)}, bf16[256,1024]{1,0:T(8,128)(2,1)S(1)}, u32[]{:S(2)}, u32[]{:S(2)}) collective-permute-start(bf16[256,1024]{1,0:T(8,128)(2,1)S(1)} %convolution_convert_fusion.1), channel_id=1, source_target_pairs={{0,1},{1,0},{2,3},{3,2},{4,5},{5,4},{6,7},{7,6},{8,9},{9,8},{10,11... | collective-permute-start | bytes 1572872 | tf_op jit(solution)/shard_map/ppermute | solution.py:358
  96.9 22.3 %collective-permute-start.3 = (bf16[256,1024]{1,0:T(8,128)(2,1)}, bf16[256,1024]{1,0:T(8,128)(2,1)}, u32[]{:S(2)}, u32[]{:S(2)}) collective-permute-start(bf16[256,1024]{1,0:T(8,128)(2,1)} %convolution_convert_fusion), channel_id=1, source_target_pairs={{0,1},{1,0},{2,3},{3,2},{4,5},{5,4},{6,7},{7,6},{8,9},{9,8},{10,11... | collective-permute-start | bytes 1572872 | tf_op jit(solution)/shard_map/ppermute | solution.py:358
  99.3 29.8 %collective-permute-start.1 = (bf16[256,1024]{1,0:T(8,128)(2,1)}, bf16[256,1024]{1,0:T(8,128)(2,1)S(1)}, u32[]{:S(2)}, u32[]{:S(2)}) collective-permute-start(bf16[256,1024]{1,0:T(8,128)(2,1)} %convolution_convert_fusion.2), channel_id=1, source_target_pairs={{0,1},{1,0},{2,3},{3,2},{4,5},{5,4},{6,7},{7,6},{8,9},{9,8},{10,11... | collective-permute-start | bytes 1572872 | tf_op jit(solution)/shard_map/ppermute | solution.py:358
  124.0 1.9 copy-start.2
  135.0 42.0 %copy-start.6 = (bf16[1,256,1024]{2,1,0:T(8,128)(2,1)S(1)}, bf16[1,256,1024]{2,1,0:T(8,128)(2,1)}, u32[]{:S(2)}) copy-start(bf16[1,256,1024]{2,1,0:T(8,128)(2,1)} %param.11) | copy-start | bytes 1572868
  228.1 3.5 %copy-start.3 = (bf16[512,4096]{1,0:T(8,128)(2,1)S(1)}, bf16[512,4096]{1,0:T(8,128)(2,1)}, u32[]{:S(2)}) copy-start(bf16[512,4096]{1,0:T(8,128)(2,1)} %shard_map.110) | copy-start | bytes 12582916
  228.1 10.8 %slice-start = ((s8[8388608]{0:T(1024)(128)(4,1)}), s8[4194304]{0:T(1024)(128)(4,1)S(1)}, s32[]{:S(2)}) async-start(s8[8388608]{0:T(1024)(128)(4,1)} %bitcast.43), calls=%async_computation.1 | async-start | bytes 8388608
  231.5 7.3 %slice-start.1 = ((s8[8388608]{0:T(1024)(128)(4,1)}), s8[4194304]{0:T(1024)(128)(4,1)S(1)}, s32[]{:S(2)}) async-start(s8[8388608]{0:T(1024)(128)(4,1)} %bitcast.43), calls=%async_computation.2 | async-start | bytes 8388608
  238.9 59.9 %copy-start.1 = (f32[32,16]{0,1:T(8,128)S(1)}, f32[32,16]{0,1:T(8,128)}, u32[]{:S(2)}) copy-start(f32[32,16]{0,1:T(8,128)} %param.17) | copy-start | bytes 6148
  244.9 51.7 %copy-start.5 = (bf16[256,1024]{1,0:T(8,128)(2,1)S(1)}, bf16[256,1024]{1,0:T(8,128)(2,1)}, u32[]{:S(2)}) copy-start(bf16[256,1024]{1,0:T(8,128)(2,1)} %add_convert_fusion.1.x_ref) | copy-start | bytes 1572868
Sparse Core Ops, SparseCore 0:
  10.2 50.5 all-gather.1

commit v4 on v3

--- a/solution.py
+++ b/solution.py
@@ -50,16 +50,22 @@
     pl.semaphore_wait(barrier, jnp.where(inner, 3, 2))
 
 
-def gather_kernel(count, pieces, x_ref, out_ref, local_sem, send_sem, z_sem, y_sem):
+def gather_kernel(count, cuts, halved, x_ref, out_ref, local_sem, send_sem, z_sem, y_sem):
     me = lax.axis_index("ma")
     row = lax.axis_index("row")
     length, width = x_ref.shape
-    step_rows = length // pieces
+    pieces = len(cuts) - 1
     greet(me, count, row)
+
+    def leaves(block):
+        return block // (count // 2) == 1 - row if halved else block >= 0
+
+    def comes(block):
+        return block // (count // 2) == row if halved else block >= 0
 
     def place(block, piece, which):
         return out_ref.at[
-            pl.ds(pl.multiple_of(which * length + piece * step_rows, step_rows), step_rows),
+            pl.ds(pl.multiple_of(which * length + cuts[piece], 16), cuts[piece + 1] - cuts[piece]),
             pl.ds(pl.multiple_of(block * width, width), width),
         ]
 
@@ -77,7 +83,7 @@
         )
 
     def own(piece):
-        return x_ref.at[pl.ds(piece * step_rows, step_rows), :]
+        return x_ref.at[pl.ds(cuts[piece], cuts[piece + 1] - cuts[piece]), :]
 
     for piece in range(pieces):
 
@@ -89,7 +95,10 @@
         def _():
             copy(1, me, piece, own(piece)).start()
 
-        copy(2, me, piece, own(piece)).start()
+        @pl.when(leaves(me))
+        def _():
+            copy(2, me, piece, own(piece)).start()
+
     mine = pltpu.make_async_copy(
         x_ref,
         out_ref.at[
@@ -111,7 +120,9 @@
                 def _():
                     copy(0, block, piece).start()
 
-                copy(2, block, piece).start()
+                @pl.when(leaves(block))
+                def _():
+                    copy(2, block, piece).start()
 
             @pl.when(me + step < count)
             def _():
@@ -122,21 +133,30 @@
                 def _():
                     copy(1, block, piece).start()
 
-                copy(2, block, piece).start()
+                @pl.when(leaves(block))
+                def _():
+                    copy(2, block, piece).start()
 
     mine.wait()
     for block in range(count):
         for piece in range(pieces):
             here = place(block, piece, 1 - row)
-            pltpu.make_async_remote_copy(
+            arrival = pltpu.make_async_remote_copy(
                 src_ref=here,
                 dst_ref=here,
                 send_sem=send_sem.at[2, block, piece],
                 recv_sem=y_sem.at[block, piece],
                 device_id={"row": 1 - row},
                 device_id_type=MESH,
-            ).wait_recv()
-            copy(2, block, piece).wait_send()
+            )
+
+            @pl.when(comes(jnp.int32(block)))
+            def _():
+                arrival.wait_recv()
+
+            @pl.when(leaves(jnp.int32(block)))
+            def _():
+                copy(2, block, piece).wait_send()
 
             @pl.when(jnp.logical_and(me < count - 1, block <= me))
             def _():
@@ -147,10 +167,11 @@
                 copy(1, block, piece).wait_send()
 
 
-def gather_all(values, count, pieces, collective_id):
+def gather_all(values, count, cuts, halved, collective_id):
     length, width = values.shape
+    pieces = len(cuts) - 1
     return pl.pallas_call(
-        functools.partial(gather_kernel, count, pieces),
+        functools.partial(gather_kernel, count, cuts, halved),
         out_shape=jax.ShapeDtypeStruct((2 * length, count * width), values.dtype),
         in_specs=[pl.BlockSpec(memory_space=pltpu.VMEM)],
         out_specs=pl.BlockSpec(memory_space=pltpu.VMEM),
@@ -334,22 +355,37 @@
     swap = [(i, i ^ 1) for i in range(row_count)]
     my_row = lax.axis_index("row")
     ba_count = lax.axis_size("ba")
-    lane = lax.axis_index("ba") % 2
-    half_rows = attention_output_matrix.shape[0] // 2
-    out_piece = lax.dynamic_slice_in_dim(attention_output_matrix, lane * half_rows, half_rows, 0)
-    out_other = lax.ppermute(out_piece, "row", swap)
-    out_rest = lax.ppermute(out_other, "ba", [(i, i ^ 1) for i in range(ba_count)])
+    lane = lax.axis_index("ba") % 4
+    piece_rows = attention_output_matrix.shape[0] // 4
+    out_piece = lax.dynamic_slice_in_dim(attention_output_matrix, lane * piece_rows, piece_rows, 0)
+    out_piece = lax.ppermute(out_piece, "row", swap)
+    out_across = lax.ppermute(out_piece, "ba", [(i, i ^ 2) for i in range(ba_count)])
+    core_swap = [(i, i ^ 1) for i in range(ba_count)]
+    out_pieces = [out_piece, lax.ppermute(out_piece, "ba", core_swap), out_across]
+    out_pieces.append(lax.ppermute(out_across, "ba", core_swap))
     gains = jnp.concatenate(
         [attn_gain.reshape(1, part_width), ffn_gain.reshape(1, part_width)]
         + [jnp.zeros((14, part_width), jnp.bfloat16)]
     )
-    whole = lax.all_gather(jnp.concatenate([token_rows, gains]), "ma", axis=1, tiled=True)
-    whole_rows = whole[:slab_rows]
+    padded = slab_rows + gains.shape[0]
+    gathered = gather_all(
+        jnp.concatenate([token_rows, gains]), ma_count, (0, slab_rows // 2, padded), True, 3
+    )
+    whole = lax.dynamic_slice_in_dim(gathered, my_row * padded, padded, 0)
     ffn_gain_full = whole[slab_rows + 1]
-    normed = rms_scale(whole_rows.astype(jnp.float32), whole[slab_rows])
-    mine = lax.dynamic_slice_in_dim(normed, my_row * half, half, 1)
-    theirs = lax.dynamic_slice_in_dim(normed, (1 - my_row) * half, half, 1)
-    arrived = lax.ppermute(theirs, "row", swap)
+    own_float = whole[:slab_rows].astype(jnp.float32)
+    scale = lax.rsqrt(jnp.mean(own_float * own_float, axis=-1, keepdims=True) + epsilon)
+    gain_half = lax.dynamic_slice_in_dim(whole[slab_rows], my_row * half, half, 0)
+
+    def with_gain(rows):
+        return (rows.astype(jnp.float32) * gain_half.astype(jnp.float32)).astype(jnp.bfloat16)
+
+    mine = with_gain(lax.dynamic_slice(whole, (0, my_row * half), (slab_rows, half)))
+    arrived = with_gain(
+        lax.dynamic_slice(
+            gathered, ((1 - my_row) * padded, my_row * half), (slab_rows, half)
+        )
+    )
     weights_qkv = (query_weight, key_weight, value_projection_matrix)
     outgoing = [
         jnp.dot(arrived, matrix, preferred_element_type=jnp.float32).astype(jnp.bfloat16)
@@ -357,7 +393,7 @@
     ]
     incoming = [lax.ppermute(part, "row", swap) for part in outgoing]
     projected = [
-        jnp.dot(mine, matrix, preferred_element_type=jnp.float32) + part.astype(jnp.float32)
+        (jnp.dot(mine, matrix, preferred_element_type=jnp.float32) + part.astype(jnp.float32)) * scale
         for matrix, part in zip(weights_qkv, incoming)
     ]
     query_heads, key_heads, value_heads = [
@@ -381,11 +417,11 @@
         "shqk,skhd->sqhd", weights, value_heads, preferred_element_type=jnp.float32
     )
     attended = attended.astype(jnp.bfloat16).reshape(slab_rows, inner_width)
-    out_far = jnp.where(
-        lane == 0,
-        jnp.concatenate([out_other, out_rest]),
-        jnp.concatenate([out_rest, out_other]),
-    )
+    out_far = jnp.zeros_like(attention_output_matrix)
+    for offset, member in enumerate(out_pieces):
+        out_far = lax.dynamic_update_slice_in_dim(
+            out_far, member, (lane ^ offset) * piece_rows, 0
+        )
     out_full = jnp.where(
         my_row == 0,
         jnp.concatenate([attention_output_matrix, out_far], axis=1),
@@ -395,7 +431,9 @@
     residual_stream = (token_float + attn_out).astype(jnp.bfloat16)
     residual_f = residual_stream.astype(jnp.float32)
     gate_full, up_full, down_full = (gate_weight, up_weight, down_projection_weight)
-    group_rows = gather_all(residual_stream, ma_count, 2, 0)
+    group_rows = gather_all(
+        residual_stream, ma_count, (0, slab_rows // 2, slab_rows), False, 0
+    )
     ffn_in = rms_scale(group_rows.astype(jnp.float32), ffn_gain_full)
     gate_act = jnp.dot(ffn_in, gate_full, preferred_element_type=jnp.float32)
     up_act = jnp.dot(ffn_in, up_full, preferred_element_type=jnp.float32)

time: 306 us -> 301 us (0.984)
  waiting for transfers between devices: 65.5 us -> 8.74 us
  Pallas kernels: 143 us -> 194 us
  matrix products: 35.3 us -> 50.6 us
  between operations: 13.7 us -> 0.27 us
  other arithmetic: 27.6 us -> 20.2 us
  local copies, waits for them, and re-layouts: 12.5 us -> 17 us
    pallas_call x1 -> x2, Pallas kernels: 48.9 us -> 97.7 us  [gather_all(): pl.pallas_call(functools.partial(gather_kernel, count, cuts, halved), out...]
    ppermute x3 -> x4, waiting for transfers between devices: 45.1 us -> 3.35 us  [the longest x1 3.34 us: on_device(): lax.ppermute(out_piece, 'ba', [(i, i ^ 2) for i in range(ba_count)])]
    ppermute x3, waiting for transfers between devices: 20.3 us -> 5.39 us  [on_device(): incoming = [lax.ppermute(part, 'row', swap) for part in outgoing]]
    dot_general x3, matrix products: 4.89 us -> 13.1 us  [on_device(): jnp.dot(mine, matrix, preferred_element_type=jnp.float32)]
    dot_general x3, matrix products: 5.4 us -> 11.5 us  [on_device(): jnp.dot(arrived, matrix, preferred_element_type=jnp.float32)]
    select_n x1 -> x0, other arithmetic: 4.05 us -> none  [on_device(): jnp.where(lane == 0, jnp.concatenate([out_other, out_rest]), jnp.concaten...]
    convert_element_type x4 -> x0, other arithmetic: 4.03 us -> none  [the longest x1 2.22 us: rms_scale(): (values * lax.rsqrt(mean_square + epsilon) * gain.astype(jnp.float32)).as...]
  transfers between devices with their start and end apart: 7 -> 7, of which waited for: 6 -> 3; matrix products, arithmetic and copies ran while one was open for 14% -> 19% of each run, Pallas kernels for 0% -> 16%
where the time goes in v4:
time: 301 us; the launch traced here: 300 us
  Pallas kernels  194 us (64%)
  matrix products  50.6 us (17%)
  other arithmetic  20.2 us (7%)
  local copies, waits for them, and re-layouts  17 us (6%)
  starting transfers between devices  9.12 us (3%)
  waiting for transfers between devices  8.74 us (3%)
    pallas_call x2, Pallas kernels, gather_all(): pl.pallas_call(functools.partial(gather_kernel, count, cuts, halved), out...  97.7 us
    pallas_call x2, Pallas kernels, reduce_all(): pl.pallas_call(functools.partial(reduce_kernel, count, pieces, paired), o...  96.1 us
    dot_general x3, matrix products, on_device(): jnp.dot(mine, matrix, preferred_element_type=jnp.float32)  13.1 us
    dot_general x3, matrix products, on_device(): jnp.dot(arrived, matrix, preferred_element_type=jnp.float32)  11.5 us
    dot_general x1, matrix products, on_device(): gate_act = jnp.dot(ffn_in, gate_full, preferred_element_type=jnp.float32)  7.22 us
  transfers between devices with their start and end apart: 7, of which 3 were waited for; matrix products, arithmetic and copies ran while one was open for 19% of the time, Pallas kernels for 16%

profile of v4, /device:TPU:0, one launch (start us, length us, event | category | flops | bytes accessed | tf_op | source)
XLA Modules:
  0.0 299.8 jit_solution(12059832093436537249)
XLA Ops:
  1.3 3.1 %collective-permute-start.3 = (bf16[256,2048]{1,0:T(8,128)(2,1)S(1)}, bf16[256,2048]{1,0:T(8,128)(2,1)S(1)}, u32[]{:S(2)}, u32[]{:S(2)}) collective-permute-start(bf16[256,2048]{1,0:T(8,128)(2,1)S(1)} %constant_dynamic-slice_fusion), channel_id=1, source_target_pairs={{0,1},{1,0},{2,3},{3,2},{4,5},{5,4},{6,7},{7,6},{8,9},{9,8},{10,11... | collective-permute-start | bytes 3145736 | tf_op jit(solution)/shard_map/ppermute | solution.py:361
  5.8 2.0 maximum_maximum_fusion.x_ref
  7.8 48.2 %shard_map.109 = bf16[544,4096]{1,0:T(8,128)(2,1)} custom-call(bf16[272,1024]{1,0:T(8,128)(2,1)} %maximum_maximum_fusion.x_ref), custom_call_target="tpu_custom_call" | custom-call | tf_op jit(solution)/shard_map/pallas_call | solution.py:173
  57.0 4.8 %convolution_convert_fusion.2 = bf16[256,1024]{1,0:T(8,128)(2,1)} fusion(bf16[2048,1024]{1,0:T(8,128)(2,1)} %param.15, bf16[544,4096]{1,0:T(8,128)(2,1)} %shard_map.109, s32[]{:T(128)S(6)} %select_n.55, s32[]{:T(128)S(6)} %select_n.53, f32[2048]{0:T(1024)S(1)} %bitcast.39), kind=kOutput, calls=%fused_computation.30 | convolution fusion | flops 1075576832 | bytes 5775368 | tf_op jit(solution)/shard_map/dot_general | solution.py:391
  61.9 2.5 collective-permute-start
  64.3 3.3 %convolution_convert_fusion = bf16[256,1024]{1,0:T(8,128)(2,1)} fusion(bf16[2048,1024]{1,0:T(8,128)(2,1)S(1)} %copy-done.8, bf16[544,4096]{1,0:T(8,128)(2,1)} %shard_map.109, s32[]{:T(128)S(6)} %select_n.55, s32[]{:T(128)S(6)} %select_n.53, f32[2048]{0:T(1024)S(1)} %bitcast.40), kind=kOutput, calls=%fused_computation.28 | convolution fusion | flops 1075576832 | bytes 5775368 | tf_op jit(solution)/shard_map/dot_general | solution.py:391
  67.8 3.3 %convolution_convert_fusion.1 = bf16[256,1024]{1,0:T(8,128)(2,1)} fusion(bf16[2048,1024]{1,0:T(8,128)(2,1)S(1)} %copy-done.9, bf16[544,4096]{1,0:T(8,128)(2,1)} %shard_map.109, s32[]{:T(128)S(6)} %select_n.55, s32[]{:T(128)S(6)} %select_n.53, f32[2048]{0:T(1024)S(1)} %bitcast.41), kind=kOutput, calls=%fused_computation.29 | convolution fusion | flops 1075576832 | bytes 5775368 | tf_op jit(solution)/shard_map/dot_general | solution.py:391
  71.2 1.9 collective-permute-start.1
  74.2 2.1 multiply_reduce_fusion
  76.3 4.3 %fusion.4 = f32[256,256,16]{1,2,0:T(8,128)} fusion(s32[256,256]{1,0:T(8,128)S(1)} %fusion.25, f32[32,16]{0,1:T(8,128)S(1)} %copy-done), kind=kOutput, calls=%fused_computation.8 | convolution fusion | flops 404750336 | bytes 4458496 | tf_op jit(solution)/shard_map/dmy,du->umy/dot_general | solution.py:406
  80.6 5.3 %copy.21 = f32[256,256,16]{0,1,2:T(8,128)} copy(f32[256,256,16]{1,2,0:T(8,128)} %fusion.4) | data formatting | bytes 8388608 | tf_op jit(solution)/shard_map/dmy,du->umy/dot_general | solution.py:406
  85.9 2.6 collective-permute-done.2
  88.6 4.8 %multiply_convert_fusion.2 = bf16[256,1024]{1,0:T(8,128)(2,1)} fusion(bf16[256,1024]{1,0:T(8,128)(2,1)S(1)} %collective-permute-done.2, bf16[2048,1024]{1,0:T(8,128)(2,1)} %param.14, f32[2048]{0:T(1024)S(1)} %bitcast.42, bf16[544,4096]{1,0:T(8,128)(2,1)} %shard_map.109, s32[]{:T(128)S(6)} %select_n.52, s32[]{:T(128)S(6)} %select_n.54, ...), kind=kOutput, calls=%fused_computation.34 | convolution fusion | flops 1076363264 | bytes 6300680 | tf_op jit(solution)/shard_map/dot_general | solution.py:396
  93.3 1.5 collective-permute-start.5
  94.8 2.7 collective-permute-done.1
  97.6 3.6 %multiply_convert_fusion.3 = bf16[256,1024]{1,0:T(8,128)(2,1)} fusion(bf16[256,1024]{1,0:T(8,128)(2,1)} %collective-permute-done.1, bf16[2048,1024]{1,0:T(8,128)(2,1)S(1)} %copy-done.10, f32[2048]{0:T(1024)S(1)} %bitcast.43, bf16[544,4096]{1,0:T(8,128)(2,1)} %shard_map.109, s32[]{:T(128)S(6)} %select_n.52, s32[]{:T(128)S(6)} %select_n.54, ...), kind=kOutput, calls=%fused_computation.35 | convolution fusion | flops 1076363264 | bytes 6300680 | tf_op jit(solution)/shard_map/dot_general | solution.py:396
  102.6 3.1 %bitcast_add_fusion = f32[16,256,256]{1,2,0:T(8,128)S(1)} fusion(f32[256,256,16]{0,1,2:T(8,128)} %copy.21, bf16[256,16,64]{0,2,1:T(8,128)(2,1)S(1)} %bitcast.33, bf16[256,16,64]{0,2,1:T(8,128)(2,1)S(1)} %bitcast.32), kind=kOutput, calls=%fused_computation.9 | convolution fusion | flops 135266304 | bytes 9437184 | tf_op jit(solution)/shard_map/sqhd,skhd->shqk/dot_general | solution.py:410
  106.1 4.7 %multiply_convert_fusion.4 = bf16[256,1024]{1,0:T(8,128)(2,1)} fusion(bf16[256,1024]{1,0:T(8,128)(2,1)} %collective-permute-done, bf16[2048,1024]{1,0:T(8,128)(2,1)S(1)} %copy-done.11, f32[2048]{0:T(1024)S(1)} %bitcast.44, bf16[544,4096]{1,0:T(8,128)(2,1)} %shard_map.109, s32[]{:T(128)S(6)} %select_n.52, s32[]{:T(128)S(6)} %select_n.54, ...), kind=kOutput, calls=%fused_computation.36 | convolution fusion | flops 1076363264 | bytes 6300680 | tf_op jit(solution)/shard_map/dot_general | solution.py:396
  110.8 3.3 %collective-permute-done.5 = bf16[256,2048]{1,0:T(8,128)(2,1)S(1)} collective-permute-done((bf16[256,2048]{1,0:T(8,128)(2,1)S(1)}, bf16[256,2048]{1,0:T(8,128)(2,1)S(1)}, u32[]{:S(2)}, u32[]{:S(2)}) %collective-permute-start.5) | collective-permute-done | bytes 1048608 | tf_op jit(solution)/shard_map/ppermute | solution.py:362
  114.9 2.1 copy.18
  117.0 5.5 %fusion.16 = bf16[16,64,256]{2,1,0:T(8,128)(2,1)} fusion(bf16[256,16,64]{0,2,1:T(8,128)(2,1)} %bitcast.35, f32[16,256]{1,0:T(8,128)S(1)} %fusion.46, f32[16,256,256]{1,2,0:T(8,128)} %copy-done.2), kind=kOutput, calls=%fused_computation.27 | convolution fusion | flops 137629952 | bytes 5259264 | tf_op jit(solution)/shard_map/shqk,skhd->sqhd/dot_general | solution.py:416
  122.4 2.0 copy.23.left_ref
  125.3 1.5 constant_dynamic-update-slice_fusion
  127.5 5.5 %maximum_select_fusion.right_ref = bf16[1024,4096]{1,0:T(8,128)(2,1)} fusion(bf16[1024,2048]{1,0:T(8,128)(2,1)S(1)} %constant_dynamic-update-slice_fusion, bf16[1024,2048]{1,0:T(8,128)(2,1)S(1)} %copy-done.4, pred[]{:T(512)S(6)} %eq.21), kind=kLoop, calls=%fused_computation.6 | loop fusion | flops 37748736 | bytes 16777216 | tf_op jit(solution)/shard_map/jit(_where)/select_n | solution.py:425
  133.1 44.8 %shard_map.110 = f32[256,1024]{1,0:T(8,128)} custom-call(bf16[256,1024]{1,0:T(8,128)(2,1)} %copy.23.left_ref, bf16[1024,4096]{1,0:T(8,128)(2,1)} %maximum_select_fusion.right_ref), custom_call_target="tpu_custom_call" | custom-call | tf_op jit(solution)/shard_map/pallas_call | solution.py:317
  177.9 2.2 add_convert_fusion.1.x_ref
  180.1 49.5 %shard_map.111 = bf16[512,4096]{1,0:T(8,128)(2,1)} custom-call(bf16[256,1024]{1,0:T(8,128)(2,1)} %add_convert_fusion.1.x_ref), custom_call_target="tpu_custom_call" | custom-call | tf_op jit(solution)/shard_map/pallas_call | solution.py:173
  229.6 3.2 %fusion.1 = f32[512]{0:T(512)S(1)} fusion(bf16[512,4096]{1,0:T(8,128)(2,1)} %shard_map.111), kind=kLoop, calls=%fused_computation.3 | loop fusion | flops 6290944 | bytes 4196352 | tf_op jit(solution)/shard_map/reduce_sum | solution.py:28
  233.0 7.2 %fusion.18 = f32[512,1024]{1,0:T(8,128)S(1)} fusion(bf16[4096,1024]{1,0:T(8,128)(2,1)} %param.19, bf16[512,4096]{1,0:T(8,128)(2,1)S(1)} %copy-done.3, f32[4096]{0:T(1024)S(1)} %bitcast.37, f32[512]{0:T(512)S(1)} %add_rsqrt_fusion), kind=kOutput, calls=%fused_computation.31 | convolution fusion | flops 4303355904 | bytes 14698496 | tf_op jit(solution)/shard_map/dot_general | solution.py:438
  240.3 6.0 %fusion.14.left_ref = bf16[512,1024]{1,0:T(8,128)(2,1)} fusion(f32[512,1024]{1,0:T(8,128)S(1)} %fusion.18, bf16[4096,1024]{1,0:T(8,128)(2,1)S(1)} %bitcast.46, bf16[512,4096]{1,0:T(8,128)(2,1)S(1)} %copy-done.3, f32[4096]{0:T(1024)S(1)} %bitcast.38, f32[512]{0:T(512)S(1)} %add_rsqrt_fusion), kind=kOutput, calls=%fused_computation.23 | convolution fusion | flops 4308598784 | bytes 15747072 | tf_op jit(solution)/shard_map/dot_general | solution.py:439
  246.3 51.3 %shard_map.112 = f32[256,1024]{1,0:T(8,128)} custom-call(bf16[512,1024]{1,0:T(8,128)(2,1)} %fusion.14.left_ref, bf16[1024,4096]{1,0:T(8,128)(2,1)} %right_ref.1), custom_call_target="tpu_custom_call" | custom-call | tf_op jit(solution)/shard_map/pallas_call | solution.py:317
  297.6 2.2 fusion.23
  (53 shorter events, 9.4 us)
Async XLA Ops:
  0.0 76.3 %copy-start = (f32[32,16]{0,1:T(8,128)S(1)}, f32[32,16]{0,1:T(8,128)}, u32[]{:S(2)}) copy-start(f32[32,16]{0,1:T(8,128)} %param.17) | copy-start | bytes 6148
  1.3 92.0 %collective-permute-start.3 = (bf16[256,2048]{1,0:T(8,128)(2,1)S(1)}, bf16[256,2048]{1,0:T(8,128)(2,1)S(1)}, u32[]{:S(2)}, u32[]{:S(2)}) collective-permute-start(bf16[256,2048]{1,0:T(8,128)(2,1)S(1)} %constant_dynamic-slice_fusion), channel_id=1, source_target_pairs={{0,1},{1,0},{2,3},{3,2},{4,5},{5,4},{6,7},{7,6},{8,9},{9,8},{10,11... | collective-permute-start | bytes 3145736 | tf_op jit(solution)/shard_map/ppermute | solution.py:361
  56.0 8.3 %copy-start.8 = (bf16[2048,1024]{1,0:T(8,128)(2,1)S(1)}, bf16[2048,1024]{1,0:T(8,128)(2,1)}, u32[]{:S(2)}) copy-start(bf16[2048,1024]{1,0:T(8,128)(2,1)} %param.14) | copy-start | bytes 12582916
  61.9 6.0 %copy-start.9 = (bf16[2048,1024]{1,0:T(8,128)(2,1)S(1)}, bf16[2048,1024]{1,0:T(8,128)(2,1)}, u32[]{:S(2)}) copy-start(bf16[2048,1024]{1,0:T(8,128)(2,1)} %param.13) | copy-start | bytes 12582916
  61.9 44.0 %collective-permute-start = (bf16[256,1024]{1,0:T(8,128)(2,1)}, bf16[256,1024]{1,0:T(8,128)(2,1)}, u32[]{:S(2)}, u32[]{:S(2)}) collective-permute-start(bf16[256,1024]{1,0:T(8,128)(2,1)} %convolution_convert_fusion.2), channel_id=1, source_target_pairs={{0,1},{1,0},{2,3},{3,2},{4,5},{5,4},{6,7},{7,6},{8,9},{9,8},{10,11... | collective-permute-start | bytes 1572872 | tf_op jit(solution)/shard_map/ppermute | solution.py:394
  67.7 20.9 %collective-permute-start.2 = (bf16[256,1024]{1,0:T(8,128)(2,1)}, bf16[256,1024]{1,0:T(8,128)(2,1)S(1)}, u32[]{:S(2)}, u32[]{:S(2)}) collective-permute-start(bf16[256,1024]{1,0:T(8,128)(2,1)} %convolution_convert_fusion), channel_id=1, source_target_pairs={{0,1},{1,0},{2,3},{3,2},{4,5},{5,4},{6,7},{7,6},{8,9},{9,8},{10,11... | collective-permute-start | bytes 1572872 | tf_op jit(solution)/shard_map/ppermute | solution.py:394
  71.2 26.4 %collective-permute-start.1 = (bf16[256,1024]{1,0:T(8,128)(2,1)}, bf16[256,1024]{1,0:T(8,128)(2,1)}, u32[]{:S(2)}, u32[]{:S(2)}) collective-permute-start(bf16[256,1024]{1,0:T(8,128)(2,1)} %convolution_convert_fusion.1), channel_id=1, source_target_pairs={{0,1},{1,0},{2,3},{3,2},{4,5},{5,4},{6,7},{7,6},{8,9},{9,8},{10,11... | collective-permute-start | bytes 1572872 | tf_op jit(solution)/shard_map/ppermute | solution.py:394
  85.9 11.7 %copy-start.10 = (bf16[2048,1024]{1,0:T(8,128)(2,1)S(1)}, bf16[2048,1024]{1,0:T(8,128)(2,1)}, u32[]{:S(2)}) copy-start(bf16[2048,1024]{1,0:T(8,128)(2,1)} %param.13) | copy-start | bytes 12582916
  93.3 7.8 %copy-start.7 = (bf16[256,1024]{1,0:T(8,128)(2,1)S(1)}, bf16[256,1024]{1,0:T(8,128)(2,1)}, u32[]{:S(2)}) copy-start(bf16[256,1024]{1,0:T(8,128)(2,1)} %multiply_convert_fusion.2) | copy-start | bytes 1572868
  93.3 20.8 %collective-permute-start.5 = (bf16[256,2048]{1,0:T(8,128)(2,1)S(1)}, bf16[256,2048]{1,0:T(8,128)(2,1)S(1)}, u32[]{:S(2)}, u32[]{:S(2)}) collective-permute-start(bf16[256,2048]{1,0:T(8,128)(2,1)S(1)} %collective-permute-done.3), channel_id=1, source_target_pairs={{0,16},{8,24},{16,0},{24,8},{1,17},{9,25},{17,1},{25,9},{2,18},{10... | collective-permute-start | bytes 3145736 | tf_op jit(solution)/shard_map/ppermute | solution.py:362
  102.6 3.5 %copy-start.11 = (bf16[2048,1024]{1,0:T(8,128)(2,1)S(1)}, bf16[2048,1024]{1,0:T(8,128)(2,1)}, u32[]{:S(2)}) copy-start(bf16[2048,1024]{1,0:T(8,128)(2,1)} %param.15) | copy-start | bytes 12582916
  105.7 8.4 %copy-start.2 = (f32[16,256,256]{1,2,0:T(8,128)}, f32[16,256,256]{1,2,0:T(8,128)S(1)}, u32[]{:S(2)}) copy-start(f32[16,256,256]{1,2,0:T(8,128)S(1)} %bitcast_add_fusion) | copy-start | bytes 12582916
  105.7 19.4 %collective-permute-start.4 = (bf16[256,2048]{1,0:T(8,128)(2,1)S(1)}, bf16[256,2048]{1,0:T(8,128)(2,1)S(1)}, u32[]{:S(2)}, u32[]{:S(2)}) collective-permute-start(bf16[256,2048]{1,0:T(8,128)(2,1)S(1)} %collective-permute-done.3), channel_id=1, source_target_pairs={{0,8},{8,0},{16,24},{24,16},{1,9},{9,1},{17,25},{25,17},{2,10},{10... | collective-permute-start | bytes 3145736 | tf_op jit(solution)/shard_map/ppermute | solution.py:364
  114.1 11.2 %collective-permute-start.6 = (bf16[256,2048]{1,0:T(8,128)(2,1)S(1)}, bf16[256,2048]{1,0:T(8,128)(2,1)}, u32[]{:S(2)}, u32[]{:S(2)}) collective-permute-start(bf16[256,2048]{1,0:T(8,128)(2,1)S(1)} %collective-permute-done.5), channel_id=1, source_target_pairs={{0,8},{8,0},{16,24},{24,16},{1,9},{9,1},{17,25},{25,17},{2,10},{10... | collective-permute-start | bytes 3145736 | tf_op jit(solution)/shard_map/ppermute | solution.py:365
  125.0 2.5 copy-start.4
  133.1 44.8 %copy-start.6 = (bf16[1,256,1024]{2,1,0:T(8,128)(2,1)S(1)}, bf16[1,256,1024]{2,1,0:T(8,128)(2,1)}, u32[]{:S(2)}) copy-start(bf16[1,256,1024]{2,1,0:T(8,128)(2,1)} %param.11) | copy-start | bytes 1572868
  229.6 3.5 %copy-start.3 = (bf16[512,4096]{1,0:T(8,128)(2,1)S(1)}, bf16[512,4096]{1,0:T(8,128)(2,1)}, u32[]{:S(2)}) copy-start(bf16[512,4096]{1,0:T(8,128)(2,1)} %shard_map.111) | copy-start | bytes 12582916
  229.6 10.7 %slice-start = ((s8[8388608]{0:T(1024)(128)(4,1)}), s8[4194304]{0:T(1024)(128)(4,1)S(1)}, s32[]{:S(2)}) async-start(s8[8388608]{0:T(1024)(128)(4,1)} %bitcast.45), calls=%async_computation | async-start | bytes 8388608
  233.0 7.2 %slice-start.1 = ((s8[8388608]{0:T(1024)(128)(4,1)}), s8[4194304]{0:T(1024)(128)(4,1)S(1)}, s32[]{:S(2)}) async-start(s8[8388608]{0:T(1024)(128)(4,1)} %bitcast.45), calls=%async_computation.1 | async-start | bytes 8388608
  240.3 59.5 %copy-start.1 = (f32[32,16]{0,1:T(8,128)S(1)}, f32[32,16]{0,1:T(8,128)}, u32[]{:S(2)}) copy-start(f32[32,16]{0,1:T(8,128)} %param.17) | copy-start | bytes 6148
  246.3 51.3 %copy-start.5 = (bf16[256,1024]{1,0:T(8,128)(2,1)S(1)}, bf16[256,1024]{1,0:T(8,128)(2,1)}, u32[]{:S(2)}) copy-start(bf16[256,1024]{1,0:T(8,128)(2,1)} %add_convert_fusion.1.x_ref) | copy-start | bytes 1572868
